TPU v7x, 32 devices: a whole 2x2x4 slice. The times are simulated.
32 devices in a mesh: mp: 8 (over z, x), dp: 4 (over y, core).
Axes of the slice: x: 2, y: 2, z: 4, core: 2. Of those that a mesh axis runs over, the one named last changes fastest.
Arguments:
- tables: bfloat16 [20, 16384, 128], P(None, 'mp'), may hold values from -3 to 3
- block_rows: int32 [2048, 128], P(('mp', 'dp')), may hold values from 0 to 2047
- block_slots: int32 [2048, 128], P(('mp', 'dp')), may hold values from 0 to 127
- block_table: int32 [2048], P(('mp', 'dp')), may hold values from 0 to 19
- block_peer: int32 [2048, 1], P(('mp', 'dp')), may hold values from 0 to 7; in each aligned block of 64 rows (0 to 63, 64 to 127, ...) at most 16 rows name the same one
- block_len: int32 [2048], P(('mp', 'dp')), may hold values from 1 to 128
- block_count: int32 [32], P(('mp', 'dp')), may hold values from 1 to 64, as said below
- cross_in: bfloat16 [4, 2560, 256], P(None, 'dp'), may hold values from -0.23632812 to 0.23632812
- cross_mix: bfloat16 [4, 256, 256], replicated, may hold values from -0.5625 to 0.5625
- cross_out: bfloat16 [4, 256, 2560], P(None, None, 'dp'), may hold values from -0.375 to 0.375
- cross_bias: float32 [4, 2560], replicated, may hold values from -3 to 3
- gate_weight: bfloat16 [4, 2560], replicated, may hold values from -0.47265625 to 0.47265625
Outputs:
- crossed: bfloat16 [4096, 2560], P(('mp', 'dp'))
Inputs may be any that keep to these rules, and one draw needn't show every extreme that they name: `block_peer`: in the 64 blocks of one device no destination is named by more than 16 blocks, a bound that the blocks of some device reach. The live blocks of a device are its first block_count blocks; some device has exactly 64. Entries of a block at positions below its block_len are live. `block_rows`: A row index within the device's own shard of the table. `block_slots`: A sample of the destination device.
All inputs are finite; a program needn't handle non-finite values.
Results may differ from a plain program's by a relative error of at most 0.0059.
Values may be sent and summed in bfloat16 or wider, within the bound.
A program may use at most 128 MiB of HBM per device.

v0:
```python
import functools

import jax
import jax.numpy as jnp
from jax import lax
from jax.experimental import pallas as pl
from jax.experimental.pallas import tpu as pltpu
from jax.sharding import PartitionSpec as P

B_DEV = 128
UNROLL = 8
STREAMS = 4
MESH = pl.DeviceIdType.MESH
POOL_LIMIT = 30 << 20
CROSS_LIMIT = 34 << 20
VMEM_LIMIT = 67043328


def pool_kernel(
    unroll,
    count_ref,
    table_hbm,
    peer_hbm,
    len_hbm,
    rows_hbm,
    slots_hbm,
    tables_hbm,
    out_ref,
    table_ref,
    peer_ref,
    len_ref,
    rows_ref,
    slots_ref,
    tables_ref,
    acc,
    slot_of,
    key_of,
    ready,
    small_sem,
    table_sem,
):
    table_count, rows_dev, width = tables_ref.shape
    total_blocks, block = rows_ref.shape
    tiles, samples, _ = out_ref.shape
    pairs = (
        (table_hbm, table_ref),
        (peer_hbm, peer_ref),
        (len_hbm, len_ref),
        (rows_hbm, rows_ref),
        (slots_hbm, slots_ref),
    )
    small = [pltpu.make_async_copy(a, b, small_sem.at[i]) for i, (a, b) in enumerate(pairs)]
    for copy in small:
        copy.start()

    def table_copy(t):
        return pltpu.make_async_copy(tables_hbm.at[t], tables_ref.at[t], table_sem.at[t])

    for t in range(table_count):
        table_copy(t).start()
        ready[t] = 0

    def need(t):
        @pl.when(ready[t] == 0)
        def _():
            table_copy(t).wait()
            ready[t] = 1

    def clear(i, carry):
        out_ref[i] = jnp.zeros((samples, width), jnp.bfloat16)
        slot_of[i] = -1
        return carry

    lax.fori_loop(0, tiles, clear, 0)
    for copy in small:
        copy.wait()
    count = count_ref[0]

    lane = lax.broadcasted_iota(jnp.int32, (block, 128), 1)
    sample = lax.broadcasted_iota(jnp.int32, (samples, block), 0)
    entry = lax.broadcasted_iota(jnp.int32, (samples, block), 1)

    def group(g, used):
        made = []
        for u in range(unroll):
            need(table_ref[g * unroll + u])
        for u in range(unroll):
            b = g * unroll + u
            row = rows_ref[pl.ds(b, 1), :]
            slot = slots_ref[pl.ds(b, 1), :]
            table = table_ref[b]
            column = jnp.broadcast_to(row, (128, block)).T
            pick = jnp.concatenate(
                [
                    jnp.where(column == lane + c * 128, 1.0, 0.0).astype(jnp.bfloat16)
                    for c in range(rows_dev // 128)
                ],
                axis=1,
            )
            picked = jnp.dot(pick, tables_ref[table], preferred_element_type=jnp.float32)
            place = jnp.where((sample == slot) & (entry < len_ref[b]), 1.0, 0.0)
            made.append(
                jnp.dot(
                    place.astype(jnp.bfloat16),
                    picked.astype(jnp.bfloat16),
                    preferred_element_type=jnp.float32,
                )
            )
        for u in range(unroll):
            b = g * unroll + u
            key = peer_ref[b] * table_count + table_ref[b]
            live = b < count
            known = slot_of[key]
            first = known < 0
            at = jnp.where(live, jnp.where(first, used, known), total_blocks)
            acc[at] = jnp.where(first, made[u], acc[at] + made[u])
            slot_of[key] = jnp.where(live, at, known)
            key_of[at] = key
            used = used + jnp.where(live & first, 1, 0)
        return used

    used = lax.fori_loop(0, (count + unroll - 1) // unroll, group, 0)

    def flush(i, carry):
        out_ref[key_of[i]] = acc[i].astype(jnp.bfloat16)
        return carry

    lax.fori_loop(0, used, flush, 0)
    for t in range(table_count):
        need(t)


def pool(peers, tables, block_rows, block_slots, block_table, block_peer, block_len, block_count):
    table_count, _, width = tables.shape
    total_blocks = block_rows.shape[0]
    tiles = peers * table_count
    unroll = UNROLL if total_blocks % UNROLL == 0 else 1
    hbm = pl.BlockSpec(memory_space=pltpu.HBM)
    vmem = pl.BlockSpec(memory_space=pltpu.VMEM)
    return pl.pallas_call(
        functools.partial(pool_kernel, unroll),
        out_shape=jax.ShapeDtypeStruct((tiles, B_DEV, width), jnp.bfloat16),
        in_specs=[pl.BlockSpec(memory_space=pltpu.SMEM)] + [hbm] * 6,
        out_specs=vmem,
        scratch_shapes=[
            pltpu.SMEM((total_blocks,), jnp.int32),
            pltpu.SMEM((total_blocks,), jnp.int32),
            pltpu.SMEM((total_blocks,), jnp.int32),
            pltpu.VMEM(block_rows.shape, jnp.int32),
            pltpu.VMEM(block_slots.shape, jnp.int32),
            pltpu.VMEM(tables.shape, jnp.bfloat16),
            pltpu.VMEM((total_blocks + 1, B_DEV, width), jnp.float32),
            pltpu.SMEM((tiles,), jnp.int32),
            pltpu.SMEM((total_blocks + 1,), jnp.int32),
            pltpu.SMEM((table_count,), jnp.int32),
            pltpu.SemaphoreType.DMA((5,)),
            pltpu.SemaphoreType.DMA((table_count,)),
        ],
        compiler_params=pltpu.CompilerParams(
            vmem_limit_bytes=POOL_LIMIT if peers <= 8 else VMEM_LIMIT
        ),
        cost_estimate=pl.CostEstimate(
            flops=2 * total_blocks * B_DEV * tables.shape[1] * width,
            bytes_accessed=2 * tables.size + 2 * tiles * B_DEV * width,
            transcendentals=0,
        ),
        name="pool",
    )(
        block_count,
        *(
            pltpu.with_memory_space_constraint(x, pltpu.HBM)
            for x in (
                block_table,
                block_peer[:, 0],
                block_len,
                block_rows,
                block_slots,
                tables,
            )
        )
    )


def cross_kernel(
    peers,
    share,
    partial_ref,
    in_ref,
    far_ref,
    mix_ref,
    out_w_ref,
    bias_ref,
    gate_ref,
    result_ref,
    held,
    emb,
    win,
    wout,
    ring_send,
    ring_recv,
    w_send,
    w_recv,
    w_local,
):
    tiles, samples, width = partial_ref.shape
    table_count = tiles // peers
    part = table_count // STREAMS
    experts = mix_ref.shape[0]
    ahead_count = far_ref.shape[0]
    me = lax.axis_index("mp")
    half = peers // 2
    at = jnp.where(lax.rem(me, 2) == 0, lax.div(me, 2), peers - 1 - lax.div(me, 2))

    def member(position):
        position = lax.rem(position + 2 * peers, peers)
        return jnp.where(position < half, 2 * position, 2 * (peers - 1 - position) + 1)

    ahead, behind = member(at + 1), member(at - 1)

    barrier = pltpu.get_barrier_semaphore()
    greet = [{"mp": ahead}, {"mp": behind}]
    if share:
        d = lax.axis_index("dp")
        twin = d + 1 - 2 * lax.rem(d, 2)
        across = lax.rem(d + 2, 4)
        greet += [{"dp": twin}, {"dp": across}]
    for target in greet:
        pl.semaphore_signal(barrier, inc=1, device_id=target, device_id_type=MESH)
    pl.semaphore_wait(barrier, len(greet))

    def ring_copy(stream, source, step):
        target = ahead if stream % 2 == 0 else behind
        return pltpu.make_async_remote_copy(
            src_ref=source,
            dst_ref=held.at[step, stream],
            send_sem=ring_send.at[stream, step],
            recv_sem=ring_recv.at[stream, step],
            device_id={"mp": target},
            device_id_type=MESH,
        )

    def own_tiles(stream, distance):
        dest = member(at - distance if stream % 2 == 0 else at + distance)
        return pl.ds(dest * table_count + stream * part, part)

    for stream in range(STREAMS):
        ring_copy(stream, partial_ref.at[own_tiles(stream, 1)], 0).start()

    if share:

        def piece_refs(q, owner):
            if q < experts:
                return in_ref.at[q], win.at[owner, q]
            return out_w_ref.at[q - experts], wout.at[owner, q - experts]

        def w_copy(kind, q):
            if kind == 0:
                source, place = piece_refs(q, d)
                target = across
            elif kind == 1:
                source, place = piece_refs(q, d)
                target = twin
            else:
                _, place = piece_refs(q, across)
                source = far_ref.at[q] if q < ahead_count else place
                target = twin
            return pltpu.make_async_remote_copy(
                src_ref=source,
                dst_ref=place,
                send_sem=w_send.at[kind, q],
                recv_sem=w_recv.at[kind, q],
                device_id={"dp": target},
                device_id_type=MESH,
            )

        pieces = 2 * experts
        for q in range(ahead_count, pieces):
            w_copy(0, q).start()
        for q in range(ahead_count):
            w_copy(2, q).start()
        for q in range(pieces):
            w_copy(1, q).start()
        local = []
        for q in range(pieces):
            source, place = piece_refs(q, d)
            local.append(pltpu.make_async_copy(source, place, w_local.at[q]))
            local[-1].start()
        for q in range(ahead_count):
            _, place = piece_refs(q, across)
            local.append(pltpu.make_async_copy(far_ref.at[q], place, w_local.at[pieces + q]))
            local[-1].start()

    def hop(step, last):
        for stream in range(STREAMS):
            ring_copy(stream, held.at[step, stream], step).wait_recv()
            mine = partial_ref[own_tiles(stream, step + 2)]
            total = held[step, stream].astype(jnp.float32) + mine.astype(jnp.float32)
            total = total.astype(jnp.bfloat16)
            if last:
                for i in range(part):
                    column = (stream * part + i) * width
                    emb[:, column : column + width] = total[i]
            else:
                held[step, stream] = total
                ring_copy(stream, held.at[step, stream], step + 1).start()

    if share:
        passed = ahead_count
        for step in range(peers - 2):
            hop(step, False)
            if 1 <= step and passed < pieces:
                w_copy(0, passed).wait_recv()
                w_copy(2, passed).start()
                passed += 1
        hop(peers - 2, True)
        for q in range(passed, pieces):
            w_copy(0, q).wait_recv()
            w_copy(2, q).start()
        for copy in local:
            copy.wait()
    else:

        def turn(step, carry):
            hop(step, False)
            return carry

        lax.fori_loop(0, peers - 2, turn, 0)
        hop(peers - 2, True)

    owners = win.shape[0] if share else 1
    depth = in_ref.shape[1]
    columns = out_w_ref.shape[2]
    gate = jax.nn.sigmoid(
        lax.dot_general(
            emb[...], gate_ref[...], (((1,), (1,)), ((), ())), preferred_element_type=jnp.float32
        )
    )
    mixed = []
    for e in range(experts):
        if share:
            w_copy(1, e).wait_recv()
            w_copy(2, e).wait_recv()
        projected = jnp.zeros((samples, in_ref.shape[2]), jnp.float32)
        for o in range(owners):
            weight = win[o, e] if share else in_ref[e]
            projected += jnp.dot(
                emb[:, o * depth : (o + 1) * depth], weight, preferred_element_type=jnp.float32
            )
        hidden = jnp.tanh(projected).astype(jnp.bfloat16)
        mixed.append(
            jnp.tanh(
                jnp.dot(hidden, mix_ref[e], preferred_element_type=jnp.float32)
            ).astype(jnp.bfloat16)
        )
    if share:
        for e in range(experts):
            w_copy(1, experts + e).wait_recv()
            w_copy(2, experts + e).wait_recv()
    for o in range(owners):
        span = slice(o * columns, (o + 1) * columns)
        weighted = jnp.zeros((samples, columns), jnp.float32)
        for e in range(experts):
            weight = wout[o, e] if share else out_w_ref[e]
            grown = jnp.dot(mixed[e], weight, preferred_element_type=jnp.float32)
            weighted += gate[:, e : e + 1] * (grown + bias_ref[e : e + 1, span])
        base = emb[:, span].astype(jnp.float32)
        result_ref[:, span] = (base + base * weighted).astype(jnp.bfloat16)

    for stream in range(STREAMS):
        ring_copy(stream, partial_ref.at[own_tiles(stream, 1)], 0).wait_send()

    def sent(step, carry):
        for stream in range(STREAMS):
            ring_copy(stream, held.at[step - 1, stream], step).wait_send()
        return carry

    lax.fori_loop(1, peers - 1, sent, 0)
    if share:
        for kind in (0, 1, 2):
            for q in range(ahead_count if kind == 0 else 0, pieces):
                w_copy(kind, q).wait_send()


def shared(peers, groups, cross_out):
    return groups == 4 and cross_out.shape[2] % 128 == 0 and peers <= 8


def cross(peers, groups, partial, cross_in, far_in, cross_mix, cross_out, cross_bias, gate_weight):
    tiles, samples, width = partial.shape
    table_count = tiles // peers
    experts = cross_in.shape[0]
    share = shared(peers, groups, cross_out)
    if not share:
        cross_in = lax.all_gather(cross_in, "dp", axis=1, tiled=True)
        cross_out = lax.all_gather(cross_out, "dp", axis=2, tiled=True)
        kept = (1, 8, 128), (1, 8, 128)
    else:
        kept = (groups, *cross_in.shape), (groups, *cross_out.shape)
    vmem = pl.BlockSpec(memory_space=pltpu.VMEM)
    return pl.pallas_call(
        functools.partial(cross_kernel, peers, share),
        out_shape=jax.ShapeDtypeStruct((samples, table_count * width), jnp.bfloat16),
        in_specs=[vmem] * 7,
        out_specs=vmem,
        scratch_shapes=[
            pltpu.VMEM((peers - 1, STREAMS, table_count // STREAMS, samples, width), jnp.bfloat16),
            pltpu.VMEM((samples, table_count * width), jnp.bfloat16),
            pltpu.VMEM(kept[0], jnp.bfloat16),
            pltpu.VMEM(kept[1], jnp.bfloat16),
            pltpu.SemaphoreType.DMA((STREAMS, peers - 1)),
            pltpu.SemaphoreType.DMA((STREAMS, peers - 1)),
            pltpu.SemaphoreType.DMA((3, 2 * experts)),
            pltpu.SemaphoreType.DMA((3, 2 * experts)),
            pltpu.SemaphoreType.DMA((3 * experts,)),
        ],
        compiler_params=pltpu.CompilerParams(
            collective_id=0,
            has_side_effects=True,
            vmem_limit_bytes=CROSS_LIMIT if peers <= 8 else VMEM_LIMIT,
        ),
        name="cross",
    )(partial, cross_in, far_in, cross_mix, cross_out, cross_bias, gate_weight)


def on_device(
    tables,
    block_rows,
    block_slots,
    block_table,
    block_peer,
    block_len,
    block_count,
    cross_in,
    cross_mix,
    cross_out,
    cross_bias,
    gate_weight,
):
    peers, groups = lax.axis_size("mp"), lax.axis_size("dp")
    if shared(peers, groups, cross_out):
        far_in = lax.ppermute(cross_in[: cross_in.shape[0] - 1], "dp", [(i, (i + 2) % groups) for i in range(groups)])
    else:
        far_in = jnp.zeros((1, 8, 128), jnp.bfloat16)
    partial = pool(
        peers, tables, block_rows, block_slots, block_table, block_peer, block_len, block_count
    )
    return cross(
        peers, groups, partial, cross_in, far_in, cross_mix, cross_out, cross_bias, gate_weight
    )


def solution(mesh):
    in_specs = (
        P(None, "mp", None),
        P(("mp", "dp"), None),
        P(("mp", "dp"), None),
        P(("mp", "dp")),
        P(("mp", "dp"), None),
        P(("mp", "dp")),
        P(("mp", "dp")),
        P(None, "dp", None),
        P(),
        P(None, None, "dp"),
        P(),
        P(),
    )
    out_specs = P(("mp", "dp"), None)
    return jax.shard_map(
        on_device, mesh=mesh, in_specs=in_specs, out_specs=out_specs, check_vma=False
    )
```

profile of v0, /device:TPU:0, one launch (start us, length us, event | category | flops | bytes accessed | tf_op | source)
XLA Modules:
  0.0 87.2 jit_solution(2900505364345377632)
XLA Ops:
  0.0 1.3 %slice.3 = bf16[3,640,256]{2,1,0:T(8,128)(2,1)S(1)} slice(bf16[4,640,256]{2,1,0:T(8,128)(2,1)} %in_ref.1), slice={[0:3], [0:640], [0:256]} | slice | bytes 1966080 | tf_op jit(solution)/shard_map/slice | solution.py:441
  1.3 3.1 %collective-permute-start = (bf16[3,640,256]{2,1,0:T(8,128)(2,1)S(1)}, bf16[3,640,256]{2,1,0:T(8,128)(2,1)S(1)}, u32[]{:S(2)}, u32[]{:S(2)}) collective-permute-start(bf16[3,640,256]{2,1,0:T(8,128)(2,1)S(1)} %slice.3), channel_id=1, source_target_pairs={{0,2},{1,3},{2,0},{3,1},{4,6},{5,7},{6,4},{7,5},{8,10},{9,11},{10,... | collective-permute-start | bytes 2949128 | tf_op jit(solution)/shard_map/ppermute | solution.py:441
  5.0 0.0 copy-start
  5.0 0.0 copy-start.1
  5.0 0.0 copy-start.2
  5.0 0.0 copy-start.3
  5.0 0.0 copy-start.4
  5.0 9.1 %pool.1.partial_ref = bf16[160,128,128]{2,1,0:T(8,128)(2,1)S(1)} custom-call(s32[1]{0:T(128)S(6)} %copy.14.count_ref, s32[64]{0:T(128)} %table_hbm.1, s32[64]{0:T(128)} %bitcast.1, s32[64]{0:T(128)} %len_hbm.1, s32[64,128]{1,0:T(8,128)} %rows_hbm.1, s32[64,128]{1,0:T(8,128)} %slots_hbm.1, bf16[20,2048,128]{2,1,0:T(8,128)(2,1)} %tables_hbm.1), custom_call_target="tpu_custom_call" | custom-call | flops 4294967296 | bytes 15728640 | tf_op jit(solution)/shard_map/pool/pallas_call | solution.py:140
  14.2 11.9 %collective-permute-done.far_ref = bf16[3,640,256]{2,1,0:T(8,128)(2,1)S(1)} collective-permute-done((bf16[3,640,256]{2,1,0:T(8,128)(2,1)S(1)}, bf16[3,640,256]{2,1,0:T(8,128)(2,1)S(1)}, u32[]{:S(2)}, u32[]{:S(2)}) %collective-permute-start) | collective-permute-done | bytes 983072 | tf_op jit(solution)/shard_map/ppermute | solution.py:441
  26.1 0.0 copy-done
  26.1 0.0 copy-done.1
  26.1 0.0 copy-done.2
  26.1 0.0 copy-done.3
  26.1 0.0 copy-done.4
  26.1 60.2 %cross.1 = bf16[128,2560]{1,0:T(8,128)(2,1)S(1)} custom-call(bf16[160,128,128]{2,1,0:T(8,128)(2,1)S(1)} %pool.1.partial_ref, bf16[4,640,256]{2,1,0:T(8,128)(2,1)S(1)} %copy-done, bf16[3,640,256]{2,1,0:T(8,128)(2,1)S(1)} %collective-permute-done.far_ref, bf16[4,256,256]{2,1,0:T(8,128)(2,1)S(1)} %copy-done.2, bf16[4,256,640]{2,1,0:T(8,128)(2,1)S(1)} %copy-done.1, ...), custom_call_target="tpu_custom_call" | custom-call | tf_op jit(solution)/shard_map/cross/pallas_call | solution.py:400
  86.3 0.8 copy.15
Async XLA Ops:
  1.3 24.8 %collective-permute-start = (bf16[3,640,256]{2,1,0:T(8,128)(2,1)S(1)}, bf16[3,640,256]{2,1,0:T(8,128)(2,1)S(1)}, u32[]{:S(2)}, u32[]{:S(2)}) collective-permute-start(bf16[3,640,256]{2,1,0:T(8,128)(2,1)S(1)} %slice.3), channel_id=1, source_target_pairs={{0,2},{1,3},{2,0},{3,1},{4,6},{5,7},{6,4},{7,5},{8,10},{9,11},{10,... | collective-permute-start | bytes 2949128 | tf_op jit(solution)/shard_map/ppermute | solution.py:441
  5.0 21.1 %copy-start = (bf16[4,640,256]{2,1,0:T(8,128)(2,1)S(1)}, bf16[4,640,256]{2,1,0:T(8,128)(2,1)}, u32[]{:S(2)}) copy-start(bf16[4,640,256]{2,1,0:T(8,128)(2,1)} %in_ref.1) | copy-start | bytes 3932164
  5.0 21.1 %copy-start.1 = (bf16[4,256,640]{2,1,0:T(8,128)(2,1)S(1)}, bf16[4,256,640]{2,1,0:T(8,128)(2,1)}, u32[]{:S(2)}) copy-start(bf16[4,256,640]{2,1,0:T(8,128)(2,1)} %out_w_ref.1) | copy-start | bytes 3932164
  5.0 21.1 %copy-start.2 = (bf16[4,256,256]{2,1,0:T(8,128)(2,1)S(1)}, bf16[4,256,256]{2,1,0:T(8,128)(2,1)}, u32[]{:S(2)}) copy-start(bf16[4,256,256]{2,1,0:T(8,128)(2,1)} %mix_ref.1) | copy-start | bytes 1572868
  5.0 21.1 %copy-start.3 = (f32[4,2560]{1,0:T(4,128)S(1)}, f32[4,2560]{1,0:T(4,128)}, u32[]{:S(2)}) copy-start(f32[4,2560]{1,0:T(4,128)} %bias_ref.1) | copy-start | bytes 122884
  5.0 21.1 %copy-start.4 = (bf16[4,2560]{1,0:T(4,128)(2,1)S(1)}, bf16[4,2560]{1,0:T(4,128)(2,1)}, u32[]{:S(2)}) copy-start(bf16[4,2560]{1,0:T(4,128)(2,1)} %gate_ref.1) | copy-start | bytes 61444
where the time goes:
time: 86.7 us; the launch traced here: 87.2 us
  Pallas kernels  69.4 us (80%)
  waiting for transfers between devices  11.9 us (14%)
  starting transfers between devices  3.06 us (4%)
  local copies, waits for them, and re-layouts  2.14 us (2%)
    pallas_call x1, Pallas kernels, cross(): pl.pallas_call(functools.partial(cross_kernel, peers, share), out_shape=j...  60.2 us
    ppermute x1, waiting for transfers between devices, on_device(): lax.ppermute(cross_in[:cross_in.shape[0] - 1], 'dp', [(i, (i + 2) % group...  11.9 us
    pallas_call x1, Pallas kernels, pool(): pl.pallas_call(functools.partial(pool_kernel, unroll), out_shape=jax.Shap...  9.14 us
    ppermute x1, starting transfers between devices, on_device(): lax.ppermute(cross_in[:cross_in.shape[0] - 1], 'dp', [(i, (i + 2) % group...  3.06 us
  transfers between devices with their start and end apart: 1, of which 1 were waited for; matrix products, arithmetic and copies ran while one was open for 0% of the time, Pallas kernels for 10%

commit v1 on v0

--- a/solution.py
+++ b/solution.py
@@ -12,7 +12,8 @@
 STREAMS = 4
 MESH = pl.DeviceIdType.MESH
 POOL_LIMIT = 30 << 20
-CROSS_LIMIT = 34 << 20
+FUSED_LIMIT = 48 << 20
+FOLD = 4
 VMEM_LIMIT = 67043328
 
 
@@ -183,10 +184,8 @@
 
 def cross_kernel(
     peers,
-    share,
     partial_ref,
     in_ref,
-    far_ref,
     mix_ref,
     out_w_ref,
     bias_ref,
@@ -194,19 +193,13 @@
     result_ref,
     held,
     emb,
-    win,
-    wout,
     ring_send,
     ring_recv,
-    w_send,
-    w_recv,
-    w_local,
 ):
     tiles, samples, width = partial_ref.shape
     table_count = tiles // peers
     part = table_count // STREAMS
     experts = mix_ref.shape[0]
-    ahead_count = far_ref.shape[0]
     me = lax.axis_index("mp")
     half = peers // 2
     at = jnp.where(lax.rem(me, 2) == 0, lax.div(me, 2), peers - 1 - lax.div(me, 2))
@@ -219,11 +212,6 @@
 
     barrier = pltpu.get_barrier_semaphore()
     greet = [{"mp": ahead}, {"mp": behind}]
-    if share:
-        d = lax.axis_index("dp")
-        twin = d + 1 - 2 * lax.rem(d, 2)
-        across = lax.rem(d + 2, 4)
-        greet += [{"dp": twin}, {"dp": across}]
     for target in greet:
         pl.semaphore_signal(barrier, inc=1, device_id=target, device_id_type=MESH)
     pl.semaphore_wait(barrier, len(greet))
@@ -245,50 +233,6 @@
 
     for stream in range(STREAMS):
         ring_copy(stream, partial_ref.at[own_tiles(stream, 1)], 0).start()
-
-    if share:
-
-        def piece_refs(q, owner):
-            if q < experts:
-                return in_ref.at[q], win.at[owner, q]
-            return out_w_ref.at[q - experts], wout.at[owner, q - experts]
-
-        def w_copy(kind, q):
-            if kind == 0:
-                source, place = piece_refs(q, d)
-                target = across
-            elif kind == 1:
-                source, place = piece_refs(q, d)
-                target = twin
-            else:
-                _, place = piece_refs(q, across)
-                source = far_ref.at[q] if q < ahead_count else place
-                target = twin
-            return pltpu.make_async_remote_copy(
-                src_ref=source,
-                dst_ref=place,
-                send_sem=w_send.at[kind, q],
-                recv_sem=w_recv.at[kind, q],
-                device_id={"dp": target},
-                device_id_type=MESH,
-            )
-
-        pieces = 2 * experts
-        for q in range(ahead_count, pieces):
-            w_copy(0, q).start()
-        for q in range(ahead_count):
-            w_copy(2, q).start()
-        for q in range(pieces):
-            w_copy(1, q).start()
-        local = []
-        for q in range(pieces):
-            source, place = piece_refs(q, d)
-            local.append(pltpu.make_async_copy(source, place, w_local.at[q]))
-            local[-1].start()
-        for q in range(ahead_count):
-            _, place = piece_refs(q, across)
-            local.append(pltpu.make_async_copy(far_ref.at[q], place, w_local.at[pieces + q]))
-            local[-1].start()
 
     def hop(step, last):
         for stream in range(STREAMS):
@@ -304,30 +248,335 @@
                 held[step, stream] = total
                 ring_copy(stream, held.at[step, stream], step + 1).start()
 
-    if share:
-        passed = ahead_count
-        for step in range(peers - 2):
-            hop(step, False)
-            if 1 <= step and passed < pieces:
-                w_copy(0, passed).wait_recv()
-                w_copy(2, passed).start()
-                passed += 1
-        hop(peers - 2, True)
-        for q in range(passed, pieces):
-            w_copy(0, q).wait_recv()
-            w_copy(2, q).start()
-        for copy in local:
-            copy.wait()
-    else:
-
-        def turn(step, carry):
-            hop(step, False)
-            return carry
-
-        lax.fori_loop(0, peers - 2, turn, 0)
-        hop(peers - 2, True)
-
-    owners = win.shape[0] if share else 1
+    def turn(step, carry):
+        hop(step, False)
+        return carry
+
+    lax.fori_loop(0, peers - 2, turn, 0)
+    hop(peers - 2, True)
+
+    gate = jax.nn.sigmoid(
+        lax.dot_general(
+            emb[...], gate_ref[...], (((1,), (1,)), ((), ())), preferred_element_type=jnp.float32
+        )
+    )
+    mixed = []
+    for e in range(experts):
+        projected = jnp.dot(emb[...], in_ref[e], preferred_element_type=jnp.float32)
+        hidden = jnp.tanh(projected).astype(jnp.bfloat16)
+        mixed.append(
+            jnp.tanh(
+                jnp.dot(hidden, mix_ref[e], preferred_element_type=jnp.float32)
+            ).astype(jnp.bfloat16)
+        )
+    weighted = jnp.zeros(emb.shape, jnp.float32)
+    for e in range(experts):
+        grown = jnp.dot(mixed[e], out_w_ref[e], preferred_element_type=jnp.float32)
+        weighted += gate[:, e : e + 1] * (grown + bias_ref[e : e + 1, :])
+    base = emb[...].astype(jnp.float32)
+    result_ref[...] = (base + base * weighted).astype(jnp.bfloat16)
+
+    for stream in range(STREAMS):
+        ring_copy(stream, partial_ref.at[own_tiles(stream, 1)], 0).wait_send()
+
+    def sent(step, carry):
+        for stream in range(STREAMS):
+            ring_copy(stream, held.at[step - 1, stream], step).wait_send()
+        return carry
+
+    lax.fori_loop(1, peers - 1, sent, 0)
+
+
+def plan_kernel(
+    peers,
+    count_ref,
+    table_hbm,
+    peer_hbm,
+    len_hbm,
+    rows_hbm,
+    slots_hbm,
+    rows_out,
+    slots_out,
+    index_ref,
+    table_ref,
+    peer_ref,
+    len_ref,
+    rows_ref,
+    slots_ref,
+    near_ref,
+    small_sem,
+):
+    blocks, block = rows_out.shape
+    tiles = index_ref.shape[0] - 2 * blocks
+    table_count = tiles // peers
+    part = table_count // STREAMS
+    pairs = (
+        (table_hbm, table_ref),
+        (peer_hbm, peer_ref),
+        (len_hbm, len_ref),
+        (rows_hbm, rows_ref),
+        (slots_hbm, slots_ref),
+    )
+    small = [pltpu.make_async_copy(a, b, small_sem.at[i]) for i, (a, b) in enumerate(pairs)]
+    for copy in small:
+        copy.start()
+    me = lax.axis_index("mp")
+    at = jnp.where(lax.rem(me, 2) == 0, lax.div(me, 2), peers - 1 - lax.div(me, 2))
+
+    def clear(i, carry):
+        index_ref[2 * blocks + i] = blocks
+        return carry
+
+    lax.fori_loop(0, tiles, clear, 0, unroll=8)
+    for copy in small:
+        copy.wait()
+    count = count_ref[0]
+
+    def look(b, found):
+        peer = peer_ref[b]
+        place = jnp.where(lax.rem(peer, 2) == 0, lax.div(peer, 2), peers - 1 - lax.div(peer, 2))
+        forward = lax.rem(lax.div(table_ref[b], part), 2) == 0
+        away = jnp.where(forward, at - place, place - at)
+        near = (b < count) & ((away == 1) | (away == 1 - peers))
+        near = jnp.where(near, 1, 0)
+        near_ref[b] = near
+        return found + near
+
+    found = lax.fori_loop(0, blocks, look, 0, unroll=8)
+    lane = lax.broadcasted_iota(jnp.int32, (1, block), 1)
+
+    def settle(b, carry):
+        low, high = carry
+        near = near_ref[b]
+        table = table_ref[b]
+        live = b < count
+        spot = jnp.where(near == 1, low, high)
+        rows_out[pl.ds(spot, 1), :] = rows_ref[pl.ds(b, 1), :]
+        length = jnp.where(live, len_ref[b], 0)
+        slots_out[pl.ds(spot, 1), :] = jnp.where(lane < length, slots_ref[pl.ds(b, 1), :], -1)
+        index_ref[spot] = table
+        key = 2 * blocks + peer_ref[b] * table_count + table
+        known = index_ref[key]
+        index_ref[blocks + spot] = jnp.where(live, known, blocks)
+        index_ref[key] = jnp.where(live, spot, known)
+        return low + near, high + 1 - near
+
+    lax.fori_loop(0, blocks, settle, (0, found), unroll=4)
+
+
+def plan(peers, table_count, block_rows, block_slots, block_table, block_peer, block_len, block_count):
+    blocks = block_rows.shape[0]
+    hbm = pl.BlockSpec(memory_space=pltpu.HBM)
+    vmem = pl.BlockSpec(memory_space=pltpu.VMEM)
+    smem = pl.BlockSpec(memory_space=pltpu.SMEM)
+    return pl.pallas_call(
+        functools.partial(plan_kernel, peers),
+        out_shape=(
+            jax.ShapeDtypeStruct(block_rows.shape, jnp.int32),
+            jax.ShapeDtypeStruct(block_slots.shape, jnp.int32),
+            jax.ShapeDtypeStruct((2 * blocks + peers * table_count,), jnp.int32),
+        ),
+        in_specs=[smem] + [hbm] * 5,
+        out_specs=(vmem, vmem, smem),
+        scratch_shapes=[
+            pltpu.SMEM((blocks,), jnp.int32),
+            pltpu.SMEM((blocks,), jnp.int32),
+            pltpu.SMEM((blocks,), jnp.int32),
+            pltpu.VMEM(block_rows.shape, jnp.int32),
+            pltpu.VMEM(block_slots.shape, jnp.int32),
+            pltpu.SMEM((blocks,), jnp.int32),
+            pltpu.SemaphoreType.DMA((5,)),
+        ],
+        name="plan",
+    )(
+        block_count,
+        *(
+            pltpu.with_memory_space_constraint(x, pltpu.HBM)
+            for x in (block_table, block_peer[:, 0], block_len, block_rows, block_slots)
+        )
+    )
+
+
+def fused_kernel(
+    peers,
+    near_blocks,
+    index_ref,
+    rows_ref,
+    slots_ref,
+    tables_hbm,
+    in_ref,
+    out_w_ref,
+    mix_ref,
+    bias_ref,
+    gate_ref,
+    result_ref,
+    tables_ref,
+    made_ref,
+    first,
+    held,
+    emb,
+    win,
+    wout,
+    table_sem,
+    ring_send,
+    ring_recv,
+    w_send,
+    w_recv,
+    w_local,
+):
+    table_count, rows_dev, width = tables_ref.shape
+    blocks, block = rows_ref.shape
+    samples = result_ref.shape[0]
+    part = table_count // STREAMS
+    experts = mix_ref.shape[0]
+    pieces = 2 * experts
+    me = lax.axis_index("mp")
+    half = peers // 2
+    at = jnp.where(lax.rem(me, 2) == 0, lax.div(me, 2), peers - 1 - lax.div(me, 2))
+    d = lax.axis_index("dp")
+    twin = d + 1 - 2 * lax.rem(d, 2)
+    across = lax.rem(d + 2, 4)
+
+    def member(position):
+        position = lax.rem(position + 2 * peers, peers)
+        return jnp.where(position < half, 2 * position, 2 * (peers - 1 - position) + 1)
+
+    ahead, behind = member(at + 1), member(at - 1)
+
+    table_copies = [
+        pltpu.make_async_copy(tables_hbm.at[t], tables_ref.at[t], table_sem.at[t])
+        for t in range(table_count)
+    ]
+    for copy in table_copies:
+        copy.start()
+
+    barrier = pltpu.get_barrier_semaphore()
+    greet = [{"mp": ahead}, {"mp": behind}, {"dp": twin}, {"dp": across}]
+    for target in greet:
+        pl.semaphore_signal(barrier, inc=1, device_id=target, device_id_type=MESH)
+    made_ref[blocks] = jnp.zeros((samples, width), jnp.float32)
+    pl.semaphore_wait(barrier, len(greet))
+
+    def piece_refs(q, owner):
+        if q < experts:
+            return in_ref.at[q], win.at[owner, q]
+        return out_w_ref.at[q - experts], wout.at[owner, q - experts]
+
+    def w_copy(kind, q):
+        source, place = piece_refs(q, across if kind == 2 else d)
+        return pltpu.make_async_remote_copy(
+            src_ref=place if kind == 2 else source,
+            dst_ref=place,
+            send_sem=w_send.at[kind, q],
+            recv_sem=w_recv.at[kind, q],
+            device_id={"dp": across if kind == 0 else twin},
+            device_id_type=MESH,
+        )
+
+    for q in range(pieces):
+        w_copy(0, q).start()
+
+    def ring_copy(stream, source, step):
+        target = ahead if stream % 2 == 0 else behind
+        return pltpu.make_async_remote_copy(
+            src_ref=source,
+            dst_ref=held.at[step, stream],
+            send_sem=ring_send.at[stream, step],
+            recv_sem=ring_recv.at[stream, step],
+            device_id={"mp": target},
+            device_id_type=MESH,
+        )
+
+    def own_tile(stream, distance, i):
+        dest = member(at - distance if stream % 2 == 0 else at + distance)
+        return made_ref[index_ref[2 * blocks + dest * table_count + stream * part + i]]
+
+    fold = FOLD if rows_dev % (FOLD * 128) == 0 else 1
+    depth_rows = rows_dev // fold
+    lane = lax.broadcasted_iota(jnp.int32, (block, 128), 1)
+    sample = lax.broadcasted_iota(jnp.int32, (samples, block), 0)
+
+    def group(g, carry):
+        made = []
+        for u in range(UNROLL):
+            b = g * UNROLL + u
+            table = index_ref[b]
+            column = jnp.broadcast_to(rows_ref[pl.ds(b, 1), :], (128, block)).T
+            low = lax.rem(column, depth_rows)
+            high = lax.div(column, depth_rows)
+            pick = jnp.concatenate(
+                [
+                    jnp.where(low == lane + c * 128, 1.0, 0.0).astype(jnp.bfloat16)
+                    for c in range(depth_rows // 128)
+                ],
+                axis=1,
+            )
+            side = jnp.concatenate(
+                [tables_ref[table, j * depth_rows : (j + 1) * depth_rows, :] for j in range(fold)],
+                axis=1,
+            )
+            wide = jnp.dot(pick, side, preferred_element_type=jnp.float32)
+            picked = wide[:, :width]
+            for j in range(1, fold):
+                picked = jnp.where(high == j, wide[:, j * width : (j + 1) * width], picked)
+            place = jnp.where(sample == slots_ref[pl.ds(b, 1), :], 1.0, 0.0)
+            made.append(
+                jnp.dot(
+                    place.astype(jnp.bfloat16),
+                    picked.astype(jnp.bfloat16),
+                    preferred_element_type=jnp.float32,
+                )
+            )
+        for u in range(UNROLL):
+            b = g * UNROLL + u
+            made_ref[b] = made[u] + made_ref[index_ref[blocks + b]]
+        return carry
+
+    for copy in table_copies:
+        copy.wait()
+    lax.fori_loop(0, near_blocks // UNROLL, group, 0)
+    for stream in range(STREAMS):
+        for i in range(part):
+            first[stream, i] = own_tile(stream, 1, i).astype(jnp.bfloat16)
+        ring_copy(stream, first.at[stream], 0).start()
+    for q in range(pieces):
+        w_copy(1, q).start()
+    local = []
+    for q in range(pieces):
+        source, place = piece_refs(q, d)
+        local.append(pltpu.make_async_copy(source, place, w_local.at[q]))
+        local[-1].start()
+    lax.fori_loop(near_blocks // UNROLL, blocks // UNROLL, group, 0)
+
+    def hop(step, last):
+        for stream in range(STREAMS):
+            ring_copy(stream, held.at[step, stream], step).wait_recv()
+            for i in range(part):
+                total = held[step, stream, i].astype(jnp.float32) + own_tile(stream, step + 2, i)
+                total = total.astype(jnp.bfloat16)
+                if last:
+                    column = (stream * part + i) * width
+                    emb[:, column : column + width] = total
+                else:
+                    held[step, stream, i] = total
+            if not last:
+                ring_copy(stream, held.at[step, stream], step + 1).start()
+
+    passed = 0
+    for step in range(peers - 2):
+        hop(step, False)
+        if passed < pieces:
+            w_copy(0, passed).wait_recv()
+            w_copy(2, passed).start()
+            passed += 1
+    hop(peers - 2, True)
+    for q in range(passed, pieces):
+        w_copy(0, q).wait_recv()
+        w_copy(2, q).start()
+    for copy in local:
+        copy.wait()
+
+    owners = win.shape[0]
     depth = in_ref.shape[1]
     columns = out_w_ref.shape[2]
     gate = jax.nn.sigmoid(
@@ -337,14 +586,12 @@
     )
     mixed = []
     for e in range(experts):
-        if share:
-            w_copy(1, e).wait_recv()
-            w_copy(2, e).wait_recv()
+        w_copy(1, e).wait_recv()
+        w_copy(2, e).wait_recv()
         projected = jnp.zeros((samples, in_ref.shape[2]), jnp.float32)
         for o in range(owners):
-            weight = win[o, e] if share else in_ref[e]
             projected += jnp.dot(
-                emb[:, o * depth : (o + 1) * depth], weight, preferred_element_type=jnp.float32
+                emb[:, o * depth : (o + 1) * depth], win[o, e], preferred_element_type=jnp.float32
             )
         hidden = jnp.tanh(projected).astype(jnp.bfloat16)
         mixed.append(
@@ -352,22 +599,20 @@
                 jnp.dot(hidden, mix_ref[e], preferred_element_type=jnp.float32)
             ).astype(jnp.bfloat16)
         )
-    if share:
-        for e in range(experts):
-            w_copy(1, experts + e).wait_recv()
-            w_copy(2, experts + e).wait_recv()
+    for e in range(experts):
+        w_copy(1, experts + e).wait_recv()
+        w_copy(2, experts + e).wait_recv()
     for o in range(owners):
         span = slice(o * columns, (o + 1) * columns)
         weighted = jnp.zeros((samples, columns), jnp.float32)
         for e in range(experts):
-            weight = wout[o, e] if share else out_w_ref[e]
-            grown = jnp.dot(mixed[e], weight, preferred_element_type=jnp.float32)
+            grown = jnp.dot(mixed[e], wout[o, e], preferred_element_type=jnp.float32)
             weighted += gate[:, e : e + 1] * (grown + bias_ref[e : e + 1, span])
         base = emb[:, span].astype(jnp.float32)
         result_ref[:, span] = (base + base * weighted).astype(jnp.bfloat16)
 
     for stream in range(STREAMS):
-        ring_copy(stream, partial_ref.at[own_tiles(stream, 1)], 0).wait_send()
+        ring_copy(stream, first.at[stream], 0).wait_send()
 
     def sent(step, carry):
         for stream in range(STREAMS):
@@ -375,51 +620,96 @@
         return carry
 
     lax.fori_loop(1, peers - 1, sent, 0)
-    if share:
-        for kind in (0, 1, 2):
-            for q in range(ahead_count if kind == 0 else 0, pieces):
-                w_copy(kind, q).wait_send()
+    for kind in (0, 1, 2):
+        for q in range(pieces):
+            w_copy(kind, q).wait_send()
+
+
+def fused(
+    peers,
+    groups,
+    tables,
+    block_rows,
+    block_slots,
+    block_table,
+    block_peer,
+    block_len,
+    block_count,
+    cross_in,
+    cross_mix,
+    cross_out,
+    cross_bias,
+    gate_weight,
+):
+    table_count, _, width = tables.shape
+    blocks = block_rows.shape[0]
+    experts = cross_in.shape[0]
+    rows, slots, index = plan(
+        peers, table_count, block_rows, block_slots, block_table, block_peer, block_len, block_count
+    )
+    near_blocks = min(blocks, -(-4 * blocks // peers // UNROLL) * UNROLL)
+    part = table_count // STREAMS
+    hbm = pl.BlockSpec(memory_space=pltpu.HBM)
+    vmem = pl.BlockSpec(memory_space=pltpu.VMEM)
+    smem = pl.BlockSpec(memory_space=pltpu.SMEM)
+    far = [pltpu.with_memory_space_constraint(x, pltpu.HBM) for x in (tables, cross_in, cross_out)]
+    return pl.pallas_call(
+        functools.partial(fused_kernel, peers, near_blocks),
+        out_shape=jax.ShapeDtypeStruct((B_DEV, table_count * width), jnp.bfloat16),
+        in_specs=[smem, vmem, vmem, hbm, hbm, hbm, vmem, vmem, vmem],
+        out_specs=vmem,
+        scratch_shapes=[
+            pltpu.VMEM(tables.shape, jnp.bfloat16),
+            pltpu.VMEM((blocks + 1, B_DEV, width), jnp.float32),
+            pltpu.VMEM((STREAMS, part, B_DEV, width), jnp.bfloat16),
+            pltpu.VMEM((peers - 1, STREAMS, part, B_DEV, width), jnp.bfloat16),
+            pltpu.VMEM((B_DEV, table_count * width), jnp.bfloat16),
+            pltpu.VMEM((groups, *cross_in.shape), jnp.bfloat16),
+            pltpu.VMEM((groups, *cross_out.shape), jnp.bfloat16),
+            pltpu.SemaphoreType.DMA((table_count,)),
+            pltpu.SemaphoreType.DMA((STREAMS, peers - 1)),
+            pltpu.SemaphoreType.DMA((STREAMS, peers - 1)),
+            pltpu.SemaphoreType.DMA((3, 2 * experts)),
+            pltpu.SemaphoreType.DMA((3, 2 * experts)),
+            pltpu.SemaphoreType.DMA((2 * experts,)),
+        ],
+        compiler_params=pltpu.CompilerParams(
+            collective_id=0,
+            has_side_effects=True,
+            vmem_limit_bytes=FUSED_LIMIT,
+        ),
+        name="fused",
+    )(index, rows, slots, *far, cross_mix, cross_bias, gate_weight)
 
 
 def shared(peers, groups, cross_out):
     return groups == 4 and cross_out.shape[2] % 128 == 0 and peers <= 8
 
 
-def cross(peers, groups, partial, cross_in, far_in, cross_mix, cross_out, cross_bias, gate_weight):
+def cross(peers, groups, partial, cross_in, cross_mix, cross_out, cross_bias, gate_weight):
     tiles, samples, width = partial.shape
     table_count = tiles // peers
-    experts = cross_in.shape[0]
-    share = shared(peers, groups, cross_out)
-    if not share:
-        cross_in = lax.all_gather(cross_in, "dp", axis=1, tiled=True)
-        cross_out = lax.all_gather(cross_out, "dp", axis=2, tiled=True)
-        kept = (1, 8, 128), (1, 8, 128)
-    else:
-        kept = (groups, *cross_in.shape), (groups, *cross_out.shape)
+    cross_in = lax.all_gather(cross_in, "dp", axis=1, tiled=True)
+    cross_out = lax.all_gather(cross_out, "dp", axis=2, tiled=True)
     vmem = pl.BlockSpec(memory_space=pltpu.VMEM)
     return pl.pallas_call(
-        functools.partial(cross_kernel, peers, share),
+        functools.partial(cross_kernel, peers),
         out_shape=jax.ShapeDtypeStruct((samples, table_count * width), jnp.bfloat16),
-        in_specs=[vmem] * 7,
+        in_specs=[vmem] * 6,
         out_specs=vmem,
         scratch_shapes=[
             pltpu.VMEM((peers - 1, STREAMS, table_count // STREAMS, samples, width), jnp.bfloat16),
             pltpu.VMEM((samples, table_count * width), jnp.bfloat16),
-            pltpu.VMEM(kept[0], jnp.bfloat16),
-            pltpu.VMEM(kept[1], jnp.bfloat16),
             pltpu.SemaphoreType.DMA((STREAMS, peers - 1)),
             pltpu.SemaphoreType.DMA((STREAMS, peers - 1)),
-            pltpu.SemaphoreType.DMA((3, 2 * experts)),
-            pltpu.SemaphoreType.DMA((3, 2 * experts)),
-            pltpu.SemaphoreType.DMA((3 * experts,)),
         ],
         compiler_params=pltpu.CompilerParams(
             collective_id=0,
             has_side_effects=True,
-            vmem_limit_bytes=CROSS_LIMIT if peers <= 8 else VMEM_LIMIT,
+            vmem_limit_bytes=VMEM_LIMIT,
         ),
         name="cross",
-    )(partial, cross_in, far_in, cross_mix, cross_out, cross_bias, gate_weight)
+    )(partial, cross_in, cross_mix, cross_out, cross_bias, gate_weight)
 
 
 def on_device(
@@ -437,15 +727,28 @@
     gate_weight,
 ):
     peers, groups = lax.axis_size("mp"), lax.axis_size("dp")
-    if shared(peers, groups, cross_out):
-        far_in = lax.ppermute(cross_in[: cross_in.shape[0] - 1], "dp", [(i, (i + 2) % groups) for i in range(groups)])
-    else:
-        far_in = jnp.zeros((1, 8, 128), jnp.bfloat16)
+    if shared(peers, groups, cross_out) and block_rows.shape[0] % UNROLL == 0:
+        return fused(
+            peers,
+            groups,
+            tables,
+            block_rows,
+            block_slots,
+            block_table,
+            block_peer,
+            block_len,
+            block_count,
+            cross_in,
+            cross_mix,
+            cross_out,
+            cross_bias,
+            gate_weight,
+        )
     partial = pool(
         peers, tables, block_rows, block_slots, block_table, block_peer, block_len, block_count
     )
     return cross(
-        peers, groups, partial, cross_in, far_in, cross_mix, cross_out, cross_bias, gate_weight
+        peers, groups, partial, cross_in, cross_mix, cross_out, cross_bias, gate_weight
     )
 
 

time: 86.7 us -> 77.2 us (0.89); the launches traced: 87.2 us -> 76.7 us
  waiting for transfers between devices: 11.9 us -> 0 us
  local copies, waits for them, and re-layouts: 2.14 us -> 5.58 us
  starting transfers between devices: 3.06 us -> 0 us
  Pallas kernels: 69.4 us -> 70.5 us
    ppermute x1 -> x0, waiting for transfers between devices: 11.9 us -> none  [on_device(): lax.ppermute(cross_in[:cross_in.shape[0] - 1], 'dp', [(i, (i + 2) % group...]
    unnamed x11 -> x13, local copies, waits for them, and re-layouts: 0.87 us -> 5.58 us
    ppermute x1 -> x0, starting transfers between devices: 3.06 us -> none  [on_device(): lax.ppermute(cross_in[:cross_in.shape[0] - 1], 'dp', [(i, (i + 2) % group...]
    slice x1 -> x0, local copies, waits for them, and re-layouts: 1.26 us -> none  [on_device(): cross_in[:cross_in.shape[0] - 1]]
    pallas_call x2, Pallas kernels: 69.4 us -> 70.5 us  [the longest x1 67.7 us: fused(): pl.pallas_call(functools.partial(fused_kernel, peers, near_blocks), out_s...]
  transfers between devices with their start and end apart: 1 -> 0, of which waited for: 1 -> 0; matrix products, arithmetic and copies ran while one was open for 0% -> 0% of each run, Pallas kernels for 10% -> 0%
where the time goes in v1:
time: 77.2 us; the launch traced here: 76.7 us
  Pallas kernels  70.5 us (91%)
  local copies, waits for them, and re-layouts  5.58 us (7%)
    pallas_call x1, Pallas kernels, fused(): pl.pallas_call(functools.partial(fused_kernel, peers, near_blocks), out_s...  67.7 us
    unnamed x13, local copies, waits for them, and re-layouts  5.58 us
    pallas_call x1, Pallas kernels, plan(): pl.pallas_call(functools.partial(plan_kernel, peers), out_shape=(jax.Shap...  2.79 us

profile of v1, /device:TPU:0, one launch (start us, length us, event | category | flops | bytes accessed | tf_op | source)
XLA Modules:
  0.0 76.7 jit_solution(13261105244201787071)
XLA Ops:
  0.7 2.8 %plan.1 = (s32[64,128]{1,0:T(8,128)}, s32[64,128]{1,0:T(8,128)}, s32[288]{0:T(512)}) custom-call(s32[1]{0:T(128)S(6)} %copy.14.count_ref, s32[64]{0:T(128)} %table_hbm.1, s32[64]{0:T(128)} %bitcast.1, s32[64]{0:T(128)} %len_hbm.1, s32[64,128]{1,0:T(8,128)} %rows_hbm.1, s32[64,128]{1,0:T(8,128)} %slots_hbm.1), custom_call_target="tpu_custom_call" | custom-call | tf_op jit(solution)/shard_map/plan/pallas_call | solution.py:372
  3.5 0.0 copy-start
  3.5 1.0 %copy-done = bf16[4,256,256]{2,1,0:T(8,128)(2,1)S(1)} copy-done((bf16[4,256,256]{2,1,0:T(8,128)(2,1)S(1)}, bf16[4,256,256]{2,1,0:T(8,128)(2,1)}, u32[]{:S(2)}) %copy-start) | copy-done | bytes 524312
  4.5 0.0 copy-start.1
  4.5 0.8 %copy-done.1 = f32[4,2560]{1,0:T(4,128)S(1)} copy-done((f32[4,2560]{1,0:T(4,128)S(1)}, f32[4,2560]{1,0:T(4,128)}, u32[]{:S(2)}) %copy-start.1) | copy-done | bytes 40984
  5.3 0.0 copy-start.2
  5.3 0.8 copy-done.2
  6.0 0.0 copy-start.3
  6.0 0.8 copy-done.3
  6.8 0.0 copy-start.4
  6.8 0.7 copy-done.4
  7.5 0.0 copy-start.5
  7.5 0.7 copy-done.5
  8.2 67.7 %fused.1 = bf16[128,2560]{1,0:T(8,128)(2,1)S(1)} custom-call(s32[288]{0:T(512)S(1)} %copy-done.5, s32[64,128]{1,0:T(8,128)S(1)} %copy-done.2, s32[64,128]{1,0:T(8,128)S(1)} %copy-done.3, bf16[20,2048,128]{2,1,0:T(8,128)(2,1)} %tables_hbm.1, bf16[4,640,256]{2,1,0:T(8,128)(2,1)} %in_ref.1, bf16[4,256,640]{2,1,0:T(8,128)(2,1)} %out_w_ref.1, ...), custom_call_target="tpu_custom_call" | custom-call | tf_op jit(solution)/shard_map/fused/pallas_call | solution.py:656
  75.9 0.8 %copy.15 = bf16[128,2560]{1,0:T(8,128)(2,1)} copy(bf16[128,2560]{1,0:T(8,128)(2,1)S(1)} %fused.1) | data formatting | bytes 1310720
Async XLA Ops:
  3.5 1.0 %copy-start = (bf16[4,256,256]{2,1,0:T(8,128)(2,1)S(1)}, bf16[4,256,256]{2,1,0:T(8,128)(2,1)}, u32[]{:S(2)}) copy-start(bf16[4,256,256]{2,1,0:T(8,128)(2,1)} %mix_ref.1) | copy-start | bytes 1572868
  4.5 0.8 %copy-start.1 = (f32[4,2560]{1,0:T(4,128)S(1)}, f32[4,2560]{1,0:T(4,128)}, u32[]{:S(2)}) copy-start(f32[4,2560]{1,0:T(4,128)} %bias_ref.1) | copy-start | bytes 122884
  5.3 0.8 copy-start.2
  6.0 0.8 copy-start.3
  6.8 0.7 copy-start.4
  7.5 0.7 copy-start.5

commit v2 on v1

--- a/solution.py
+++ b/solution.py
@@ -287,129 +287,78 @@
     lax.fori_loop(1, peers - 1, sent, 0)
 
 
-def plan_kernel(
+def order_blocks(peers, part, at, count, table, peer, length, plan_ref):
+    blocks = table.shape[1]
+    table_count = STREAMS * part
+    square = (blocks, blocks)
+    across = lax.broadcasted_iota(jnp.int32, square, 1)
+    down = lax.broadcasted_iota(jnp.int32, square, 0)
+
+    def turned(row):
+        return jnp.broadcast_to(row, square).T
+
+    def total(x):
+        return jnp.sum(x, axis=0, keepdims=True)
+
+    number = lax.broadcasted_iota(jnp.int32, (1, blocks), 1)
+    live = number < count
+    half = lax.shift_right_logical(peer, 1)
+    place = jnp.where((peer & 1) == 0, half, peers - 1 - half)
+    forward = table < part
+    for stream in range(2, STREAMS, 2):
+        forward = forward | ((table >= stream * part) & (table < (stream + 1) * part))
+    away = jnp.where(forward, at - place, place - at)
+    near = jnp.where(live & ((away == 1) | (away == 1 - peers)), 1, 0)
+    key = jnp.where(live, peer * table_count + table, -1)
+    near_down = turned(near)
+    before = down < across
+    near_rank = total(jnp.where(before, near_down, 0))
+    far_rank = total(jnp.where(before, 1 - near_down, 0))
+    found = total(near_down)
+    spot = jnp.where(near == 1, near_rank, found + far_rank)
+    chosen = turned(spot) == across
+    ordered_key = total(jnp.where(chosen, turned(key), 0))
+    ordered_down = turned(ordered_key)
+    known = jnp.where((ordered_down == ordered_key) & before, down, -1)
+    known = jnp.max(known, axis=0, keepdims=True)
+    tiles = peers * table_count
+    wanted = lax.broadcasted_iota(jnp.int32, (blocks, tiles), 1)
+    ordinal = lax.broadcasted_iota(jnp.int32, (blocks, tiles), 0)
+    key_down = jnp.broadcast_to(ordered_down[:, :1], (blocks, tiles))
+    latest = jnp.max(jnp.where(key_down == wanted, ordinal, -1), axis=0, keepdims=True)
+    plan_ref[0:1, :blocks] = total(jnp.where(chosen, down, 0))
+    plan_ref[1:2, :blocks] = total(jnp.where(chosen, turned(table), 0))
+    plan_ref[2:3, :blocks] = total(jnp.where(chosen, turned(jnp.where(live, length, 0)), 0))
+    plan_ref[3:4, :blocks] = jnp.where(known < 0, blocks, known)
+    plan_ref[4:5, :tiles] = jnp.where(latest < 0, blocks, latest)
+
+
+def fused_kernel(
     peers,
+    near_blocks,
     count_ref,
     table_hbm,
     peer_hbm,
     len_hbm,
     rows_hbm,
     slots_hbm,
-    rows_out,
-    slots_out,
-    index_ref,
-    table_ref,
-    peer_ref,
-    len_ref,
-    rows_ref,
-    slots_ref,
-    near_ref,
-    small_sem,
-):
-    blocks, block = rows_out.shape
-    tiles = index_ref.shape[0] - 2 * blocks
-    table_count = tiles // peers
-    part = table_count // STREAMS
-    pairs = (
-        (table_hbm, table_ref),
-        (peer_hbm, peer_ref),
-        (len_hbm, len_ref),
-        (rows_hbm, rows_ref),
-        (slots_hbm, slots_ref),
-    )
-    small = [pltpu.make_async_copy(a, b, small_sem.at[i]) for i, (a, b) in enumerate(pairs)]
-    for copy in small:
-        copy.start()
-    me = lax.axis_index("mp")
-    at = jnp.where(lax.rem(me, 2) == 0, lax.div(me, 2), peers - 1 - lax.div(me, 2))
-
-    def clear(i, carry):
-        index_ref[2 * blocks + i] = blocks
-        return carry
-
-    lax.fori_loop(0, tiles, clear, 0, unroll=8)
-    for copy in small:
-        copy.wait()
-    count = count_ref[0]
-
-    def look(b, found):
-        peer = peer_ref[b]
-        place = jnp.where(lax.rem(peer, 2) == 0, lax.div(peer, 2), peers - 1 - lax.div(peer, 2))
-        forward = lax.rem(lax.div(table_ref[b], part), 2) == 0
-        away = jnp.where(forward, at - place, place - at)
-        near = (b < count) & ((away == 1) | (away == 1 - peers))
-        near = jnp.where(near, 1, 0)
-        near_ref[b] = near
-        return found + near
-
-    found = lax.fori_loop(0, blocks, look, 0, unroll=8)
-    lane = lax.broadcasted_iota(jnp.int32, (1, block), 1)
-
-    def settle(b, carry):
-        low, high = carry
-        near = near_ref[b]
-        table = table_ref[b]
-        live = b < count
-        spot = jnp.where(near == 1, low, high)
-        rows_out[pl.ds(spot, 1), :] = rows_ref[pl.ds(b, 1), :]
-        length = jnp.where(live, len_ref[b], 0)
-        slots_out[pl.ds(spot, 1), :] = jnp.where(lane < length, slots_ref[pl.ds(b, 1), :], -1)
-        index_ref[spot] = table
-        key = 2 * blocks + peer_ref[b] * table_count + table
-        known = index_ref[key]
-        index_ref[blocks + spot] = jnp.where(live, known, blocks)
-        index_ref[key] = jnp.where(live, spot, known)
-        return low + near, high + 1 - near
-
-    lax.fori_loop(0, blocks, settle, (0, found), unroll=4)
-
-
-def plan(peers, table_count, block_rows, block_slots, block_table, block_peer, block_len, block_count):
-    blocks = block_rows.shape[0]
-    hbm = pl.BlockSpec(memory_space=pltpu.HBM)
-    vmem = pl.BlockSpec(memory_space=pltpu.VMEM)
-    smem = pl.BlockSpec(memory_space=pltpu.SMEM)
-    return pl.pallas_call(
-        functools.partial(plan_kernel, peers),
-        out_shape=(
-            jax.ShapeDtypeStruct(block_rows.shape, jnp.int32),
-            jax.ShapeDtypeStruct(block_slots.shape, jnp.int32),
-            jax.ShapeDtypeStruct((2 * blocks + peers * table_count,), jnp.int32),
-        ),
-        in_specs=[smem] + [hbm] * 5,
-        out_specs=(vmem, vmem, smem),
-        scratch_shapes=[
-            pltpu.SMEM((blocks,), jnp.int32),
-            pltpu.SMEM((blocks,), jnp.int32),
-            pltpu.SMEM((blocks,), jnp.int32),
-            pltpu.VMEM(block_rows.shape, jnp.int32),
-            pltpu.VMEM(block_slots.shape, jnp.int32),
-            pltpu.SMEM((blocks,), jnp.int32),
-            pltpu.SemaphoreType.DMA((5,)),
-        ],
-        name="plan",
-    )(
-        block_count,
-        *(
-            pltpu.with_memory_space_constraint(x, pltpu.HBM)
-            for x in (block_table, block_peer[:, 0], block_len, block_rows, block_slots)
-        )
-    )
-
-
-def fused_kernel(
-    peers,
-    near_blocks,
-    index_ref,
-    rows_ref,
-    slots_ref,
     tables_hbm,
     in_ref,
     out_w_ref,
+    mix_hbm,
+    bias_hbm,
+    gate_hbm,
+    result_ref,
+    table_row,
+    peer_row,
+    len_row,
+    rows_ref,
+    slots_ref,
     mix_ref,
     bias_ref,
     gate_ref,
-    result_ref,
+    plan_ref,
+    index_ref,
     tables_ref,
     made_ref,
     first,
@@ -417,6 +366,7 @@
     emb,
     win,
     wout,
+    small_sem,
     table_sem,
     ring_send,
     ring_recv,
@@ -443,11 +393,27 @@
 
     ahead, behind = member(at + 1), member(at - 1)
 
+    pairs = (
+        (table_hbm, table_row),
+        (peer_hbm, peer_row),
+        (len_hbm, len_row),
+        (rows_hbm, rows_ref),
+        (slots_hbm, slots_ref),
+        (mix_hbm, mix_ref),
+        (bias_hbm, bias_ref),
+        (gate_hbm, gate_ref),
+        (plan_ref, index_ref),
+    )
+    small = [pltpu.make_async_copy(a, b, small_sem.at[i]) for i, (a, b) in enumerate(pairs)]
+    for copy in small[:5]:
+        copy.start()
     table_copies = [
         pltpu.make_async_copy(tables_hbm.at[t], tables_ref.at[t], table_sem.at[t])
         for t in range(table_count)
     ]
     for copy in table_copies:
+        copy.start()
+    for copy in small[5:8]:
         copy.start()
 
     barrier = pltpu.get_barrier_semaphore()
@@ -476,6 +442,11 @@
     for q in range(pieces):
         w_copy(0, q).start()
 
+    for copy in small[:5]:
+        copy.wait()
+    order_blocks(peers, part, at, count_ref[0], table_row[...], peer_row[...], len_row[...], plan_ref)
+    small[8].start()
+
     def ring_copy(stream, source, step):
         target = ahead if stream % 2 == 0 else behind
         return pltpu.make_async_remote_copy(
@@ -489,21 +460,24 @@
 
     def own_tile(stream, distance, i):
         dest = member(at - distance if stream % 2 == 0 else at + distance)
-        return made_ref[index_ref[2 * blocks + dest * table_count + stream * part + i]]
-
-    fold = FOLD if rows_dev % (FOLD * 128) == 0 else 1
+        return made_ref[index_ref[4, dest * table_count + stream * part + i]]
+
+    even = rows_dev & (rows_dev - 1) == 0 and rows_dev >= FOLD * 128
+    fold = FOLD if even else 1
     depth_rows = rows_dev // fold
     lane = lax.broadcasted_iota(jnp.int32, (block, 128), 1)
     sample = lax.broadcasted_iota(jnp.int32, (samples, block), 0)
+    entry = lax.broadcasted_iota(jnp.int32, (samples, block), 1)
 
     def group(g, carry):
         made = []
         for u in range(UNROLL):
             b = g * UNROLL + u
-            table = index_ref[b]
-            column = jnp.broadcast_to(rows_ref[pl.ds(b, 1), :], (128, block)).T
-            low = lax.rem(column, depth_rows)
-            high = lax.div(column, depth_rows)
+            source = index_ref[0, b]
+            table = index_ref[1, b]
+            column = jnp.broadcast_to(rows_ref[pl.ds(source, 1), :], (128, block)).T
+            low = column & (depth_rows - 1) if even else column
+            high = lax.shift_right_logical(column, depth_rows.bit_length() - 1)
             pick = jnp.concatenate(
                 [
                     jnp.where(low == lane + c * 128, 1.0, 0.0).astype(jnp.bfloat16)
@@ -519,7 +493,8 @@
             picked = wide[:, :width]
             for j in range(1, fold):
                 picked = jnp.where(high == j, wide[:, j * width : (j + 1) * width], picked)
-            place = jnp.where(sample == slots_ref[pl.ds(b, 1), :], 1.0, 0.0)
+            slot = slots_ref[pl.ds(source, 1), :]
+            place = jnp.where((sample == slot) & (entry < index_ref[2, b]), 1.0, 0.0)
             made.append(
                 jnp.dot(
                     place.astype(jnp.bfloat16),
@@ -529,9 +504,10 @@
             )
         for u in range(UNROLL):
             b = g * UNROLL + u
-            made_ref[b] = made[u] + made_ref[index_ref[blocks + b]]
+            made_ref[b] = made[u] + made_ref[index_ref[3, b]]
         return carry
 
+    small[8].wait()
     for copy in table_copies:
         copy.wait()
     lax.fori_loop(0, near_blocks // UNROLL, group, 0)
@@ -548,6 +524,10 @@
         local[-1].start()
     lax.fori_loop(near_blocks // UNROLL, blocks // UNROLL, group, 0)
 
+    span = part * width
+    gated = [jnp.zeros((samples, experts), jnp.float32)]
+    projected = [jnp.zeros((samples, in_ref.shape[2]), jnp.float32) for _ in range(experts)]
+
     def hop(step, last):
         for stream in range(STREAMS):
             ring_copy(stream, held.at[step, stream], step).wait_recv()
@@ -561,39 +541,43 @@
                     held[step, stream, i] = total
             if not last:
                 ring_copy(stream, held.at[step, stream], step + 1).start()
-
-    passed = 0
+                continue
+            columns = slice(stream * span, (stream + 1) * span)
+            ready = emb[:, columns]
+            gated[0] += lax.dot_general(
+                ready,
+                gate_ref[:, columns],
+                (((1,), (1,)), ((), ())),
+                preferred_element_type=jnp.float32,
+            )
+            for e in range(experts):
+                projected[e] += jnp.dot(ready, win[stream, e], preferred_element_type=jnp.float32)
+
+    def forward(first_piece, end_piece):
+        for q in range(first_piece, end_piece):
+            w_copy(0, q).wait_recv()
+            w_copy(2, q).start()
+
     for step in range(peers - 2):
         hop(step, False)
-        if passed < pieces:
-            w_copy(0, passed).wait_recv()
-            w_copy(2, passed).start()
-            passed += 1
-    hop(peers - 2, True)
-    for q in range(passed, pieces):
-        w_copy(0, q).wait_recv()
-        w_copy(2, q).start()
+        forward(min(step, pieces - 1), min(step + 1, pieces - 1))
+    forward(min(peers - 2, pieces - 1), pieces - 1)
     for copy in local:
         copy.wait()
-
-    owners = win.shape[0]
-    depth = in_ref.shape[1]
-    columns = out_w_ref.shape[2]
-    gate = jax.nn.sigmoid(
-        lax.dot_general(
-            emb[...], gate_ref[...], (((1,), (1,)), ((), ())), preferred_element_type=jnp.float32
-        )
-    )
-    mixed = []
+    for copy in small[5:8]:
+        copy.wait()
     for e in range(experts):
         w_copy(1, e).wait_recv()
         w_copy(2, e).wait_recv()
-        projected = jnp.zeros((samples, in_ref.shape[2]), jnp.float32)
-        for o in range(owners):
-            projected += jnp.dot(
-                emb[:, o * depth : (o + 1) * depth], win[o, e], preferred_element_type=jnp.float32
-            )
-        hidden = jnp.tanh(projected).astype(jnp.bfloat16)
+    hop(peers - 2, True)
+    forward(pieces - 1, pieces)
+
+    owners = win.shape[0]
+    columns = out_w_ref.shape[2]
+    gate = jax.nn.sigmoid(gated[0])
+    mixed = []
+    for e in range(experts):
+        hidden = jnp.tanh(projected[e]).astype(jnp.bfloat16)
         mixed.append(
             jnp.tanh(
                 jnp.dot(hidden, mix_ref[e], preferred_element_type=jnp.float32)
@@ -644,21 +628,40 @@
     table_count, _, width = tables.shape
     blocks = block_rows.shape[0]
     experts = cross_in.shape[0]
-    rows, slots, index = plan(
-        peers, table_count, block_rows, block_slots, block_table, block_peer, block_len, block_count
-    )
     near_blocks = min(blocks, -(-4 * blocks // peers // UNROLL) * UNROLL)
     part = table_count // STREAMS
     hbm = pl.BlockSpec(memory_space=pltpu.HBM)
     vmem = pl.BlockSpec(memory_space=pltpu.VMEM)
-    smem = pl.BlockSpec(memory_space=pltpu.SMEM)
-    far = [pltpu.with_memory_space_constraint(x, pltpu.HBM) for x in (tables, cross_in, cross_out)]
+    lanes = -(-max(blocks, peers * table_count) // 128) * 128
+    operands = (
+        block_table.reshape(1, blocks),
+        block_peer.reshape(1, blocks),
+        block_len.reshape(1, blocks),
+        block_rows,
+        block_slots,
+        tables,
+        cross_in,
+        cross_out,
+        cross_mix,
+        cross_bias,
+        gate_weight,
+    )
     return pl.pallas_call(
         functools.partial(fused_kernel, peers, near_blocks),
         out_shape=jax.ShapeDtypeStruct((B_DEV, table_count * width), jnp.bfloat16),
-        in_specs=[smem, vmem, vmem, hbm, hbm, hbm, vmem, vmem, vmem],
+        in_specs=[pl.BlockSpec(memory_space=pltpu.SMEM)] + [hbm] * len(operands),
         out_specs=vmem,
         scratch_shapes=[
+            pltpu.VMEM((1, blocks), jnp.int32),
+            pltpu.VMEM((1, blocks), jnp.int32),
+            pltpu.VMEM((1, blocks), jnp.int32),
+            pltpu.VMEM(block_rows.shape, jnp.int32),
+            pltpu.VMEM(block_slots.shape, jnp.int32),
+            pltpu.VMEM(cross_mix.shape, jnp.bfloat16),
+            pltpu.VMEM(cross_bias.shape, jnp.float32),
+            pltpu.VMEM(gate_weight.shape, jnp.bfloat16),
+            pltpu.VMEM((8, lanes), jnp.int32),
+            pltpu.SMEM((8, lanes), jnp.int32),
             pltpu.VMEM(tables.shape, jnp.bfloat16),
             pltpu.VMEM((blocks + 1, B_DEV, width), jnp.float32),
             pltpu.VMEM((STREAMS, part, B_DEV, width), jnp.bfloat16),
@@ -666,6 +669,7 @@
             pltpu.VMEM((B_DEV, table_count * width), jnp.bfloat16),
             pltpu.VMEM((groups, *cross_in.shape), jnp.bfloat16),
             pltpu.VMEM((groups, *cross_out.shape), jnp.bfloat16),
+            pltpu.SemaphoreType.DMA((9,)),
             pltpu.SemaphoreType.DMA((table_count,)),
             pltpu.SemaphoreType.DMA((STREAMS, peers - 1)),
             pltpu.SemaphoreType.DMA((STREAMS, peers - 1)),
@@ -679,7 +683,7 @@
             vmem_limit_bytes=FUSED_LIMIT,
         ),
         name="fused",
-    )(index, rows, slots, *far, cross_mix, cross_bias, gate_weight)
+    )(block_count, *(pltpu.with_memory_space_constraint(x, pltpu.HBM) for x in operands))
 
 
 def shared(peers, groups, cross_out):

time: 77.2 us -> 66.8 us (0.87)
  Pallas kernels: 70.5 us -> 64.4 us
  local copies, waits for them, and re-layouts: 5.58 us -> 0.84 us
    unnamed x13 -> x1, local copies, waits for them, and re-layouts: 5.58 us -> 0.84 us
    pallas_call x1, Pallas kernels: 67.7 us -> 64.4 us  [fused(): pl.pallas_call(functools.partial(fused_kernel, peers, near_blocks), out_s...]
    pallas_call x1 -> x0, Pallas kernels: 2.79 us -> none  [plan(): pl.pallas_call(functools.partial(plan_kernel, peers), out_shape=(jax.Shap...]
where the time goes in v2:
time: 66.8 us; the launch traced here: 65.9 us
  Pallas kernels  64.4 us (96%)
  local copies, waits for them, and re-layouts  0.84 us (1%)
    pallas_call x1, Pallas kernels, fused(): pl.pallas_call(functools.partial(fused_kernel, peers, near_blocks), out_s...  64.4 us

profile of v2, /device:TPU:0, one launch (start us, length us, event | category | flops | bytes accessed | tf_op | source)
XLA Modules:
  0.0 65.9 jit_solution(14121543496015889892)
XLA Ops:
  0.7 64.4 %fused.1 = bf16[128,2560]{1,0:T(8,128)(2,1)S(1)} custom-call(s32[1]{0:T(128)S(6)} %copy.14.count_ref, s32[1,64]{1,0:T(1,128)} %bitcast.3, s32[1,64]{1,0:T(1,128)} %bitcast.4, s32[1,64]{1,0:T(1,128)} %bitcast.5, s32[64,128]{1,0:T(8,128)} %rows_hbm.1, s32[64,128]{1,0:T(8,128)} %slots_hbm.1, bf16[20,2048,128]{2,1,0:T(8,128)(2,1)} %tables_hbm.1, ...), custom_call_target="tpu_custom_call" | custom-call | tf_op jit(solution)/shard_map/fused/pallas_call | solution.py:649
  65.1 0.8 %copy.15 = bf16[128,2560]{1,0:T(8,128)(2,1)} copy(bf16[128,2560]{1,0:T(8,128)(2,1)S(1)} %fused.1) | data formatting | bytes 1310720

commit v3 on v2

--- a/solution.py
+++ b/solution.py
@@ -14,6 +14,9 @@
 POOL_LIMIT = 30 << 20
 FUSED_LIMIT = 48 << 20
 FOLD = 4
+RING = 4
+GROUP = 16
+SHARE = 320
 VMEM_LIMIT = 67043328
 
 
@@ -287,55 +290,73 @@
     lax.fori_loop(1, peers - 1, sent, 0)
 
 
-def order_blocks(peers, part, at, count, table, peer, length, plan_ref):
+def order_blocks(peers, table_count, cap, first_ahead, at, count, table, peer, length, plan_ref):
     blocks = table.shape[1]
-    table_count = STREAMS * part
-    square = (blocks, blocks)
-    across = lax.broadcasted_iota(jnp.int32, square, 1)
-    down = lax.broadcasted_iota(jnp.int32, square, 0)
+    slots = blocks + cap
+    number = lax.broadcasted_iota(jnp.int32, (1, blocks), 1)
+    before = lax.broadcasted_iota(jnp.int32, (blocks, blocks), 0) < lax.broadcasted_iota(
+        jnp.int32, (blocks, blocks), 1
+    )
 
     def turned(row):
-        return jnp.broadcast_to(row, square).T
+        size = row.shape[1]
+        return jnp.broadcast_to(row, (size, size)).T
 
     def total(x):
         return jnp.sum(x, axis=0, keepdims=True)
 
-    number = lax.broadcasted_iota(jnp.int32, (1, blocks), 1)
+    def rank(flag):
+        down = turned(flag)
+        return total(jnp.where(before, down, 0)), total(down)
+
+    def ranked(flag, first):
+        chosen, rest = jnp.where(flag & first, 1, 0), jnp.where(flag & ~first, 1, 0)
+        (early, found), (late, _) = rank(chosen), rank(rest)
+        return jnp.where(first, early, found + late)
+
     live = number < count
     half = lax.shift_right_logical(peer, 1)
     place = jnp.where((peer & 1) == 0, half, peers - 1 - half)
-    forward = table < part
-    for stream in range(2, STREAMS, 2):
-        forward = forward | ((table >= stream * part) & (table < (stream + 1) * part))
-    away = jnp.where(forward, at - place, place - at)
-    near = jnp.where(live & ((away == 1) | (away == 1 - peers)), 1, 0)
+    low = table < table_count // 2
+    away = jnp.where(low == first_ahead, at - place, place - at)
+    away = jnp.where(away < 0, away + peers, away)
     key = jnp.where(live, peer * table_count + table, -1)
-    near_down = turned(near)
-    before = down < across
-    near_rank = total(jnp.where(before, near_down, 0))
-    far_rank = total(jnp.where(before, 1 - near_down, 0))
-    found = total(near_down)
-    spot = jnp.where(near == 1, near_rank, found + far_rank)
-    chosen = turned(spot) == across
-    ordered_key = total(jnp.where(chosen, turned(key), 0))
+    order = jnp.where(low, ranked(low, live & (away == 1)), ranked(~low, live & (away == 1)))
+    over = order >= cap
+    spot = jnp.where(low, order, cap + order)
+    spot = jnp.where(over, 2 * cap + ranked(over, live & (away == 2)), spot)
+
+    slot = lax.broadcasted_iota(jnp.int32, (blocks, slots), 1)
+    chosen = turned(spot)[:, :1] == slot
+    down = lax.broadcasted_iota(jnp.int32, (blocks, slots), 0)
+
+    def settled(row):
+        return total(jnp.where(chosen, turned(row)[:, :1], 0))
+
+    ordered_key = settled(key + 1) - 1
     ordered_down = turned(ordered_key)
-    known = jnp.where((ordered_down == ordered_key) & before, down, -1)
+    earlier = lax.broadcasted_iota(jnp.int32, (slots, slots), 0)
+    later = lax.broadcasted_iota(jnp.int32, (slots, slots), 1)
+    known = jnp.where((ordered_down == ordered_key) & (earlier < later), earlier, -1)
     known = jnp.max(known, axis=0, keepdims=True)
     tiles = peers * table_count
-    wanted = lax.broadcasted_iota(jnp.int32, (blocks, tiles), 1)
-    ordinal = lax.broadcasted_iota(jnp.int32, (blocks, tiles), 0)
-    key_down = jnp.broadcast_to(ordered_down[:, :1], (blocks, tiles))
-    latest = jnp.max(jnp.where(key_down == wanted, ordinal, -1), axis=0, keepdims=True)
-    plan_ref[0:1, :blocks] = total(jnp.where(chosen, down, 0))
-    plan_ref[1:2, :blocks] = total(jnp.where(chosen, turned(table), 0))
-    plan_ref[2:3, :blocks] = total(jnp.where(chosen, turned(jnp.where(live, length, 0)), 0))
-    plan_ref[3:4, :blocks] = jnp.where(known < 0, blocks, known)
-    plan_ref[4:5, :tiles] = jnp.where(latest < 0, blocks, latest)
+    wanted = lax.broadcasted_iota(jnp.int32, (slots, tiles), 1)
+    ordinal = lax.broadcasted_iota(jnp.int32, (slots, tiles), 0)
+    latest = jnp.max(
+        jnp.where(ordered_down[:, :1] == wanted, ordinal, -1), axis=0, keepdims=True
+    )
+    plan_ref[0:1, :slots] = total(jnp.where(chosen, down, 0))
+    plan_ref[1:2, :slots] = settled(jnp.where(low, table, table - table_count // 2))
+    plan_ref[2:3, :slots] = settled(jnp.where(live, length, 0))
+    plan_ref[3:4, :slots] = jnp.where(known < 0, slots, known)
+    plan_ref[4:5, :tiles] = jnp.where(latest < 0, slots, latest)
+    plan_ref[5:6, :slots] = settled(jnp.where(low, 0, 1))
 
 
 def fused_kernel(
     peers,
-    near_blocks,
+    cap,
+    share,
     count_ref,
     table_hbm,
     peer_hbm,
@@ -359,7 +380,8 @@
     gate_ref,
     plan_ref,
     index_ref,
-    tables_ref,
+    low_ref,
+    high_ref,
     made_ref,
     first,
     held,
@@ -373,11 +395,14 @@
     w_send,
     w_recv,
     w_local,
+    half_send,
+    half_recv,
 ):
-    table_count, rows_dev, width = tables_ref.shape
+    table_count, rows_dev, width = tables_hbm.shape
     blocks, block = rows_ref.shape
+    slots = blocks + cap
     samples = result_ref.shape[0]
-    part = table_count // STREAMS
+    part = table_count // RING
     experts = mix_ref.shape[0]
     pieces = 2 * experts
     me = lax.axis_index("mp")
@@ -392,6 +417,10 @@
         return jnp.where(position < half, 2 * position, 2 * (peers - 1 - position) + 1)
 
     ahead, behind = member(at + 1), member(at - 1)
+    beside = me + 1 - 2 * lax.rem(me, 2)
+    first_ahead = lax.rem(d, 2) == 0
+    targets = jnp.where(first_ahead, ahead, behind), jnp.where(first_ahead, behind, ahead)
+    signs = jnp.where(first_ahead, 1, -1), jnp.where(first_ahead, -1, 1)
 
     pairs = (
         (table_hbm, table_row),
@@ -407,20 +436,36 @@
     small = [pltpu.make_async_copy(a, b, small_sem.at[i]) for i, (a, b) in enumerate(pairs)]
     for copy in small[:5]:
         copy.start()
+    half_tables = table_count // 2
     table_copies = [
-        pltpu.make_async_copy(tables_hbm.at[t], tables_ref.at[t], table_sem.at[t])
-        for t in range(table_count)
+        pltpu.make_async_copy(tables_hbm.at[t], place.at[t % half_tables], table_sem.at[t])
+        for place, start in ((low_ref, 0), (high_ref, half_tables))
+        for t in range(start, start + half_tables)
     ]
     for copy in table_copies:
-        copy.start()
-    for copy in small[5:8]:
-        copy.start()
-
+        copy.start(priority=1)
     barrier = pltpu.get_barrier_semaphore()
     greet = [{"mp": ahead}, {"mp": behind}, {"dp": twin}, {"dp": across}]
+    if share:
+        greet.append({"mp": beside})
     for target in greet:
         pl.semaphore_signal(barrier, inc=1, device_id=target, device_id_type=MESH)
-    made_ref[blocks] = jnp.zeros((samples, width), jnp.float32)
+    made_ref[slots] = jnp.zeros((samples, width), jnp.float32)
+    for copy in small[:5]:
+        copy.wait()
+    order_blocks(
+        peers,
+        table_count,
+        cap,
+        first_ahead,
+        at,
+        count_ref[0],
+        table_row[...],
+        peer_row[...],
+        len_row[...],
+        plan_ref,
+    )
+    small[8].start()
     pl.semaphore_wait(barrier, len(greet))
 
     def piece_refs(q, owner):
@@ -428,8 +473,32 @@
             return in_ref.at[q], win.at[owner, q]
         return out_w_ref.at[q - experts], wout.at[owner, q - experts]
 
+    depth = in_ref.shape[1]
+    mine = pl.ds(pl.multiple_of(lax.rem(me, 2) * (share // 2), 16), share // 2)
+    halves = []
+    if share:
+        there = win.at[d, 0, mine]
+        here = win.at[across, 0, mine]
+        halves = [
+            pltpu.make_async_remote_copy(
+                src_ref=source,
+                dst_ref=place,
+                send_sem=half_send.at[n],
+                recv_sem=half_recv.at[n],
+                device_id=target,
+                device_id_type=MESH,
+            )
+            for n, (source, place, target) in enumerate(
+                ((in_ref.at[0, mine], there, {"dp": across}), (here, here, {"mp": beside}))
+            )
+        ]
+        halves[0].start()
+
     def w_copy(kind, q):
         source, place = piece_refs(q, across if kind == 2 else d)
+        if kind == 0 and q == 0 and share:
+            rest = pl.ds(share, depth - share)
+            source, place = source.at[rest], place.at[rest]
         return pltpu.make_async_remote_copy(
             src_ref=place if kind == 2 else source,
             dst_ref=place,
@@ -439,16 +508,13 @@
             device_id_type=MESH,
         )
 
-    for q in range(pieces):
+    for q in range(1 if share == depth else 0, pieces):
         w_copy(0, q).start()
-
-    for copy in small[:5]:
-        copy.wait()
-    order_blocks(peers, part, at, count_ref[0], table_row[...], peer_row[...], len_row[...], plan_ref)
-    small[8].start()
+    for copy in small[5:8]:
+        copy.start()
 
     def ring_copy(stream, source, step):
-        target = ahead if stream % 2 == 0 else behind
+        target = targets[stream % 2]
         return pltpu.make_async_remote_copy(
             src_ref=source,
             dst_ref=held.at[step, stream],
@@ -458,9 +524,12 @@
             device_id_type=MESH,
         )
 
+    def base(stream):
+        return stream % 2 * (table_count // 2) + stream // 2 * part
+
     def own_tile(stream, distance, i):
-        dest = member(at - distance if stream % 2 == 0 else at + distance)
-        return made_ref[index_ref[4, dest * table_count + stream * part + i]]
+        dest = member(at - signs[stream % 2] * distance)
+        return made_ref[index_ref[4, dest * table_count + base(stream) + i]]
 
     even = rows_dev & (rows_dev - 1) == 0 and rows_dev >= FOLD * 128
     fold = FOLD if even else 1
@@ -469,10 +538,10 @@
     sample = lax.broadcasted_iota(jnp.int32, (samples, block), 0)
     entry = lax.broadcasted_iota(jnp.int32, (samples, block), 1)
 
-    def group(g, carry):
+    def group(kind, g, carry):
         made = []
-        for u in range(UNROLL):
-            b = g * UNROLL + u
+        for u in range(GROUP):
+            b = g * GROUP + u
             source = index_ref[0, b]
             table = index_ref[1, b]
             column = jnp.broadcast_to(rows_ref[pl.ds(source, 1), :], (128, block)).T
@@ -485,10 +554,19 @@
                 ],
                 axis=1,
             )
-            side = jnp.concatenate(
-                [tables_ref[table, j * depth_rows : (j + 1) * depth_rows, :] for j in range(fold)],
-                axis=1,
-            )
+            sides = []
+            for j in range(fold):
+                rows = slice(j * depth_rows, (j + 1) * depth_rows)
+                if kind == 0:
+                    sides.append(low_ref[table, rows, :])
+                elif kind == 1:
+                    sides.append(high_ref[table, rows, :])
+                else:
+                    upper = index_ref[5, b] == 1
+                    sides.append(
+                        jnp.where(upper, high_ref[table, rows, :], low_ref[table, rows, :])
+                    )
+            side = jnp.concatenate(sides, axis=1)
             wide = jnp.dot(pick, side, preferred_element_type=jnp.float32)
             picked = wide[:, :width]
             for j in range(1, fold):
@@ -502,19 +580,33 @@
                     preferred_element_type=jnp.float32,
                 )
             )
-        for u in range(UNROLL):
-            b = g * UNROLL + u
+        for u in range(GROUP):
+            b = g * GROUP + u
             made_ref[b] = made[u] + made_ref[index_ref[3, b]]
         return carry
 
+    def pool(kind, start, end):
+        work = functools.partial(group, kind)
+        lax.fori_loop(start // GROUP, end // GROUP, work, 0)
+
+    def begin(parity):
+        for stream in range(parity, RING, 2):
+            for i in range(part):
+                first[stream, i] = own_tile(stream, 1, i).astype(jnp.bfloat16)
+            ring_copy(stream, first.at[stream], 0).start()
+
     small[8].wait()
-    for copy in table_copies:
+    for copy in table_copies[:half_tables]:
         copy.wait()
-    lax.fori_loop(0, near_blocks // UNROLL, group, 0)
-    for stream in range(STREAMS):
-        for i in range(part):
-            first[stream, i] = own_tile(stream, 1, i).astype(jnp.bfloat16)
-        ring_copy(stream, first.at[stream], 0).start()
+    pool(0, 0, cap)
+    begin(0)
+    for copy in table_copies[half_tables:]:
+        copy.wait()
+    pool(1, cap, 2 * cap)
+    begin(1)
+    if share:
+        halves[0].wait_recv()
+        halves[1].start()
     for q in range(pieces):
         w_copy(1, q).start()
     local = []
@@ -522,44 +614,55 @@
         source, place = piece_refs(q, d)
         local.append(pltpu.make_async_copy(source, place, w_local.at[q]))
         local[-1].start()
-    lax.fori_loop(near_blocks // UNROLL, blocks // UNROLL, group, 0)
-
-    span = part * width
+    pool(2, 2 * cap, 4 * cap)
+
     gated = [jnp.zeros((samples, experts), jnp.float32)]
     projected = [jnp.zeros((samples, in_ref.shape[2]), jnp.float32) for _ in range(experts)]
 
     def hop(step, last):
-        for stream in range(STREAMS):
+        for stream in range(RING):
             ring_copy(stream, held.at[step, stream], step).wait_recv()
             for i in range(part):
                 total = held[step, stream, i].astype(jnp.float32) + own_tile(stream, step + 2, i)
                 total = total.astype(jnp.bfloat16)
                 if last:
-                    column = (stream * part + i) * width
+                    column = (base(stream) + i) * width
                     emb[:, column : column + width] = total
                 else:
                     held[step, stream, i] = total
             if not last:
                 ring_copy(stream, held.at[step, stream], step + 1).start()
                 continue
-            columns = slice(stream * span, (stream + 1) * span)
-            ready = emb[:, columns]
-            gated[0] += lax.dot_general(
-                ready,
-                gate_ref[:, columns],
-                (((1,), (1,)), ((), ())),
-                preferred_element_type=jnp.float32,
-            )
-            for e in range(experts):
-                projected[e] += jnp.dot(ready, win[stream, e], preferred_element_type=jnp.float32)
+            start, end = base(stream) * width, (base(stream) + part) * width
+            while start < end:
+                owner = start // depth
+                stop = min(end, (owner + 1) * depth)
+                ready = emb[:, start:stop]
+                gated[0] += lax.dot_general(
+                    ready,
+                    gate_ref[:, start:stop],
+                    (((1,), (1,)), ((), ())),
+                    preferred_element_type=jnp.float32,
+                )
+                rows = slice(start - owner * depth, stop - owner * depth)
+                for e in range(experts):
+                    projected[e] += jnp.dot(
+                        ready, win[owner, e, rows, :], preferred_element_type=jnp.float32
+                    )
+                start = stop
 
     def forward(first_piece, end_piece):
         for q in range(first_piece, end_piece):
-            w_copy(0, q).wait_recv()
+            if q == 0 and share:
+                halves[1].wait_recv()
+            if q or share < depth:
+                w_copy(0, q).wait_recv()
             w_copy(2, q).start()
 
     for step in range(peers - 2):
         hop(step, False)
+        if step == 0:
+            pool(2, 4 * cap, slots)
         forward(min(step, pieces - 1), min(step + 1, pieces - 1))
     forward(min(peers - 2, pieces - 1), pieces - 1)
     for copy in local:
@@ -570,9 +673,7 @@
         w_copy(1, e).wait_recv()
         w_copy(2, e).wait_recv()
     hop(peers - 2, True)
-    forward(pieces - 1, pieces)
-
-    owners = win.shape[0]
+
     columns = out_w_ref.shape[2]
     gate = jax.nn.sigmoid(gated[0])
     mixed = []
@@ -583,29 +684,52 @@
                 jnp.dot(hidden, mix_ref[e], preferred_element_type=jnp.float32)
             ).astype(jnp.bfloat16)
         )
+
+    def span(owner):
+        return pl.ds(pl.multiple_of(owner * columns, 128), columns)
+
+    def grown(owner, e):
+        wide = jnp.dot(mixed[e], wout[owner, e], preferred_element_type=jnp.float32)
+        return gate[:, e : e + 1] * (wide + bias_ref[e : e + 1, span(owner)])
+
+    def finish(owner, weighted):
+        base = emb[:, span(owner)].astype(jnp.float32)
+        result_ref[:, span(owner)] = (base + base * weighted).astype(jnp.bfloat16)
+
     for e in range(experts):
         w_copy(1, experts + e).wait_recv()
+    for owner in (d, twin):
+        weighted = grown(owner, 0)
+        for e in range(1, experts):
+            weighted += grown(owner, e)
+        finish(owner, weighted)
+    forward(pieces - 1, pieces)
+    for e in range(experts - 1):
         w_copy(2, experts + e).wait_recv()
-    for o in range(owners):
-        span = slice(o * columns, (o + 1) * columns)
-        weighted = jnp.zeros((samples, columns), jnp.float32)
-        for e in range(experts):
-            grown = jnp.dot(mixed[e], wout[o, e], preferred_element_type=jnp.float32)
-            weighted += gate[:, e : e + 1] * (grown + bias_ref[e : e + 1, span])
-        base = emb[:, span].astype(jnp.float32)
-        result_ref[:, span] = (base + base * weighted).astype(jnp.bfloat16)
-
-    for stream in range(STREAMS):
+    far = across + 1 - 2 * lax.rem(across, 2)
+    pair = []
+    for owner in (across, far):
+        weighted = grown(owner, 0)
+        for e in range(1, experts - 1):
+            weighted += grown(owner, e)
+        pair.append(weighted)
+    finish(across, pair[0] + grown(across, experts - 1))
+    w_copy(2, pieces - 1).wait_recv()
+    finish(far, pair[1] + grown(far, experts - 1))
+
+    for stream in range(RING):
         ring_copy(stream, first.at[stream], 0).wait_send()
 
     def sent(step, carry):
-        for stream in range(STREAMS):
+        for stream in range(RING):
             ring_copy(stream, held.at[step - 1, stream], step).wait_send()
         return carry
 
     lax.fori_loop(1, peers - 1, sent, 0)
+    for copy in halves:
+        copy.wait_send()
     for kind in (0, 1, 2):
-        for q in range(pieces):
+        for q in range(1 if kind == 0 and share == depth else 0, pieces):
             w_copy(kind, q).wait_send()
 
 
@@ -628,11 +752,13 @@
     table_count, _, width = tables.shape
     blocks = block_rows.shape[0]
     experts = cross_in.shape[0]
-    near_blocks = min(blocks, -(-4 * blocks // peers // UNROLL) * UNROLL)
-    part = table_count // STREAMS
+    cap = 2 * blocks // peers
+    depth = cross_in.shape[1]
+    share = SHARE if depth % 32 == 0 and SHARE <= depth else 0
+    part = table_count // RING
     hbm = pl.BlockSpec(memory_space=pltpu.HBM)
     vmem = pl.BlockSpec(memory_space=pltpu.VMEM)
-    lanes = -(-max(blocks, peers * table_count) // 128) * 128
+    lanes = -(-max(blocks + cap, peers * table_count) // 128) * 128
     operands = (
         block_table.reshape(1, blocks),
         block_peer.reshape(1, blocks),
@@ -647,7 +773,7 @@
         gate_weight,
     )
     return pl.pallas_call(
-        functools.partial(fused_kernel, peers, near_blocks),
+        functools.partial(fused_kernel, peers, cap, share),
         out_shape=jax.ShapeDtypeStruct((B_DEV, table_count * width), jnp.bfloat16),
         in_specs=[pl.BlockSpec(memory_space=pltpu.SMEM)] + [hbm] * len(operands),
         out_specs=vmem,
@@ -662,20 +788,23 @@
             pltpu.VMEM(gate_weight.shape, jnp.bfloat16),
             pltpu.VMEM((8, lanes), jnp.int32),
             pltpu.SMEM((8, lanes), jnp.int32),
-            pltpu.VMEM(tables.shape, jnp.bfloat16),
-            pltpu.VMEM((blocks + 1, B_DEV, width), jnp.float32),
-            pltpu.VMEM((STREAMS, part, B_DEV, width), jnp.bfloat16),
-            pltpu.VMEM((peers - 1, STREAMS, part, B_DEV, width), jnp.bfloat16),
+            pltpu.VMEM((table_count // 2, *tables.shape[1:]), jnp.bfloat16),
+            pltpu.VMEM((table_count // 2, *tables.shape[1:]), jnp.bfloat16),
+            pltpu.VMEM((blocks + cap + 1, B_DEV, width), jnp.float32),
+            pltpu.VMEM((RING, part, B_DEV, width), jnp.bfloat16),
+            pltpu.VMEM((peers - 1, RING, part, B_DEV, width), jnp.bfloat16),
             pltpu.VMEM((B_DEV, table_count * width), jnp.bfloat16),
             pltpu.VMEM((groups, *cross_in.shape), jnp.bfloat16),
             pltpu.VMEM((groups, *cross_out.shape), jnp.bfloat16),
             pltpu.SemaphoreType.DMA((9,)),
             pltpu.SemaphoreType.DMA((table_count,)),
-            pltpu.SemaphoreType.DMA((STREAMS, peers - 1)),
-            pltpu.SemaphoreType.DMA((STREAMS, peers - 1)),
+            pltpu.SemaphoreType.DMA((RING, peers - 1)),
+            pltpu.SemaphoreType.DMA((RING, peers - 1)),
             pltpu.SemaphoreType.DMA((3, 2 * experts)),
             pltpu.SemaphoreType.DMA((3, 2 * experts)),
             pltpu.SemaphoreType.DMA((2 * experts,)),
+            pltpu.SemaphoreType.DMA((2,)),
+            pltpu.SemaphoreType.DMA((2,)),
         ],
         compiler_params=pltpu.CompilerParams(
             collective_id=0,
@@ -731,7 +860,10 @@
     gate_weight,
 ):
     peers, groups = lax.axis_size("mp"), lax.axis_size("dp")
-    if shared(peers, groups, cross_out) and block_rows.shape[0] % UNROLL == 0:
+    whole_tables = tables.shape[0] % RING == 0 and cross_in.shape[1] % tables.shape[2] == 0
+    cap = 2 * block_rows.shape[0] // peers
+    even = cap % GROUP == 0 and block_rows.shape[0] == 4 * cap and whole_tables
+    if shared(peers, groups, cross_out) and even:
         return fused(
             peers,
             groups,

time: 66.8 us -> 65.3 us (0.978); the launches traced: 65.9 us -> 65.1 us
  Pallas kernels: 64.4 us -> 63.6 us
    pallas_call x1, Pallas kernels: 64.4 us -> 63.6 us  [fused(): pl.pallas_call(functools.partial(fused_kernel, peers, cap, share), out_sh...]
where the time goes in v3:
time: 65.3 us; the launch traced here: 65.1 us
  Pallas kernels  63.6 us (97%)
  local copies, waits for them, and re-layouts  0.84 us (1%)
  between operations  0.66 us (1%)
    pallas_call x1, Pallas kernels, fused(): pl.pallas_call(functools.partial(fused_kernel, peers, cap, share), out_sh...  63.6 us

profile of v3, /device:TPU:0, one launch (start us, length us, event | category | flops | bytes accessed | tf_op | source)
XLA Modules:
  0.0 65.1 jit_solution(5483123048430744696)
XLA Ops:
  0.7 63.6 %fused.1 = bf16[128,2560]{1,0:T(8,128)(2,1)S(1)} custom-call(s32[1]{0:T(128)S(6)} %copy.14.count_ref, s32[1,64]{1,0:T(1,128)} %bitcast.3, s32[1,64]{1,0:T(1,128)} %bitcast.4, s32[1,64]{1,0:T(1,128)} %bitcast.5, s32[64,128]{1,0:T(8,128)} %rows_hbm.1, s32[64,128]{1,0:T(8,128)} %slots_hbm.1, bf16[20,2048,128]{2,1,0:T(8,128)(2,1)} %tables_hbm.1, ...), custom_call_target="tpu_custom_call" | custom-call | tf_op jit(solution)/shard_map/fused/pallas_call | solution.py:775
  64.3 0.8 %copy.15 = bf16[128,2560]{1,0:T(8,128)(2,1)} copy(bf16[128,2560]{1,0:T(8,128)(2,1)S(1)} %fused.1) | data formatting | bytes 1310720

commit v4 on v3

--- a/solution.py
+++ b/solution.py
@@ -422,6 +422,12 @@
     targets = jnp.where(first_ahead, ahead, behind), jnp.where(first_ahead, behind, ahead)
     signs = jnp.where(first_ahead, 1, -1), jnp.where(first_ahead, -1, 1)
 
+    barrier = pltpu.get_barrier_semaphore()
+    greet = [{"mp": ahead}, {"mp": behind}, {"dp": twin}, {"dp": across}]
+    if share:
+        greet.append({"mp": beside})
+    for target in greet:
+        pl.semaphore_signal(barrier, inc=1, device_id=target, device_id_type=MESH)
     pairs = (
         (table_hbm, table_row),
         (peer_hbm, peer_row),
@@ -444,12 +450,6 @@
     ]
     for copy in table_copies:
         copy.start(priority=1)
-    barrier = pltpu.get_barrier_semaphore()
-    greet = [{"mp": ahead}, {"mp": behind}, {"dp": twin}, {"dp": across}]
-    if share:
-        greet.append({"mp": beside})
-    for target in greet:
-        pl.semaphore_signal(barrier, inc=1, device_id=target, device_id_type=MESH)
     made_ref[slots] = jnp.zeros((samples, width), jnp.float32)
     for copy in small[:5]:
         copy.wait()
@@ -672,6 +672,23 @@
     for e in range(experts):
         w_copy(1, e).wait_recv()
         w_copy(2, e).wait_recv()
+    for stream in range(RING):
+        ring_copy(stream, first.at[stream], 0).wait_send()
+
+    def sent(step, carry):
+        for stream in range(RING):
+            ring_copy(stream, held.at[step - 1, stream], step).wait_send()
+        return carry
+
+    lax.fori_loop(1, peers - 2, sent, 0)
+    for copy in halves:
+        copy.wait_send()
+    for q in range(1 if share == depth else 0, pieces - 1):
+        w_copy(0, q).wait_send()
+    for q in range(pieces):
+        w_copy(1, q).wait_send()
+    for q in range(pieces - 2):
+        w_copy(2, q).wait_send()
     hop(peers - 2, True)
 
     columns = out_w_ref.shape[2]
@@ -696,6 +713,7 @@
         base = emb[:, span(owner)].astype(jnp.float32)
         result_ref[:, span(owner)] = (base + base * weighted).astype(jnp.bfloat16)
 
+    forward(pieces - 1, pieces)
     for e in range(experts):
         w_copy(1, experts + e).wait_recv()
     for owner in (d, twin):
@@ -703,7 +721,6 @@
         for e in range(1, experts):
             weighted += grown(owner, e)
         finish(owner, weighted)
-    forward(pieces - 1, pieces)
     for e in range(experts - 1):
         w_copy(2, experts + e).wait_recv()
     far = across + 1 - 2 * lax.rem(across, 2)
@@ -717,20 +734,10 @@
     w_copy(2, pieces - 1).wait_recv()
     finish(far, pair[1] + grown(far, experts - 1))
 
-    for stream in range(RING):
-        ring_copy(stream, first.at[stream], 0).wait_send()
-
-    def sent(step, carry):
-        for stream in range(RING):
-            ring_copy(stream, held.at[step - 1, stream], step).wait_send()
-        return carry
-
-    lax.fori_loop(1, peers - 1, sent, 0)
-    for copy in halves:
-        copy.wait_send()
-    for kind in (0, 1, 2):
-        for q in range(1 if kind == 0 and share == depth else 0, pieces):
-            w_copy(kind, q).wait_send()
+    sent(peers - 2, 0)
+    w_copy(0, pieces - 1).wait_send()
+    w_copy(2, pieces - 2).wait_send()
+    w_copy(2, pieces - 1).wait_send()
 
 
 def fused(

time: 65.3 us -> 64.6 us (0.989)
  Pallas kernels: 63.6 us -> 62.9 us
    pallas_call x1, Pallas kernels: 63.6 us -> 62.9 us  [fused(): pl.pallas_call(functools.partial(fused_kernel, peers, cap, share), out_sh...]
where the time goes in v4:
time: 64.6 us; the launch traced here: 64.4 us
  Pallas kernels  62.9 us (97%)
  local copies, waits for them, and re-layouts  0.84 us (1%)
  between operations  0.66 us (1%)
    pallas_call x1, Pallas kernels, fused(): pl.pallas_call(functools.partial(fused_kernel, peers, cap, share), out_sh...  62.9 us

profile of v4, /device:TPU:0, one launch (start us, length us, event | category | flops | bytes accessed | tf_op | source)
XLA Modules:
  0.0 64.4 jit_solution(9405786541056413034)
XLA Ops:
  0.7 62.9 %fused.1 = bf16[128,2560]{1,0:T(8,128)(2,1)S(1)} custom-call(s32[1]{0:T(128)S(6)} %copy.14.count_ref, s32[1,64]{1,0:T(1,128)} %bitcast.3, s32[1,64]{1,0:T(1,128)} %bitcast.4, s32[1,64]{1,0:T(1,128)} %bitcast.5, s32[64,128]{1,0:T(8,128)} %rows_hbm.1, s32[64,128]{1,0:T(8,128)} %slots_hbm.1, bf16[20,2048,128]{2,1,0:T(8,128)(2,1)} %tables_hbm.1, ...), custom_call_target="tpu_custom_call" | custom-call | tf_op jit(solution)/shard_map/fused/pallas_call | solution.py:782
  63.6 0.8 %copy.15 = bf16[128,2560]{1,0:T(8,128)(2,1)} copy(bf16[128,2560]{1,0:T(8,128)(2,1)S(1)} %fused.1) | data formatting | bytes 1310720

commit v5 on v4

--- a/solution.py
+++ b/solution.py
@@ -404,7 +404,7 @@
     samples = result_ref.shape[0]
     part = table_count // RING
     experts = mix_ref.shape[0]
-    pieces = 2 * experts
+    pieces = 2 * experts + 1
     me = lax.axis_index("mp")
     half = peers // 2
     at = jnp.where(lax.rem(me, 2) == 0, lax.div(me, 2), peers - 1 - lax.div(me, 2))
@@ -471,7 +471,11 @@
     def piece_refs(q, owner):
         if q < experts:
             return in_ref.at[q], win.at[owner, q]
-        return out_w_ref.at[q - experts], wout.at[owner, q - experts]
+        if q < 2 * experts - 1:
+            return out_w_ref.at[q - experts], wout.at[owner, q - experts]
+        rank = out_w_ref.shape[1] // 2
+        rows = pl.ds((q - 2 * experts + 1) * rank, rank)
+        return out_w_ref.at[experts - 1, rows], wout.at[owner, experts - 1, rows]
 
     depth = in_ref.shape[1]
     mine = pl.ds(pl.multiple_of(lax.rem(me, 2) * (share // 2), 16), share // 2)
@@ -663,8 +667,8 @@
         hop(step, False)
         if step == 0:
             pool(2, 4 * cap, slots)
-        forward(min(step, pieces - 1), min(step + 1, pieces - 1))
-    forward(min(peers - 2, pieces - 1), pieces - 1)
+        forward(min(step, pieces - 2), min(step + 1, pieces - 2))
+    forward(min(peers - 2, pieces - 2), pieces - 2)
     for copy in local:
         copy.wait()
     for copy in small[5:8]:
@@ -683,11 +687,11 @@
     lax.fori_loop(1, peers - 2, sent, 0)
     for copy in halves:
         copy.wait_send()
-    for q in range(1 if share == depth else 0, pieces - 1):
+    for q in range(1 if share == depth else 0, pieces - 2):
         w_copy(0, q).wait_send()
     for q in range(pieces):
         w_copy(1, q).wait_send()
-    for q in range(pieces - 2):
+    for q in range(pieces - 3):
         w_copy(2, q).wait_send()
     hop(peers - 2, True)
 
@@ -713,9 +717,9 @@
         base = emb[:, span(owner)].astype(jnp.float32)
         result_ref[:, span(owner)] = (base + base * weighted).astype(jnp.bfloat16)
 
-    forward(pieces - 1, pieces)
-    for e in range(experts):
-        w_copy(1, experts + e).wait_recv()
+    forward(pieces - 2, pieces)
+    for q in range(experts, pieces):
+        w_copy(1, q).wait_recv()
     for owner in (d, twin):
         weighted = grown(owner, 0)
         for e in range(1, experts):
@@ -731,13 +735,15 @@
             weighted += grown(owner, e)
         pair.append(weighted)
     finish(across, pair[0] + grown(across, experts - 1))
-    w_copy(2, pieces - 1).wait_recv()
+    for q in range(pieces - 2, pieces):
+        w_copy(2, q).wait_recv()
     finish(far, pair[1] + grown(far, experts - 1))
 
     sent(peers - 2, 0)
-    w_copy(0, pieces - 1).wait_send()
-    w_copy(2, pieces - 2).wait_send()
-    w_copy(2, pieces - 1).wait_send()
+    for q in range(pieces - 2, pieces):
+        w_copy(0, q).wait_send()
+    for q in range(pieces - 3, pieces):
+        w_copy(2, q).wait_send()
 
 
 def fused(
@@ -807,9 +813,9 @@
             pltpu.SemaphoreType.DMA((table_count,)),
             pltpu.SemaphoreType.DMA((RING, peers - 1)),
             pltpu.SemaphoreType.DMA((RING, peers - 1)),
-            pltpu.SemaphoreType.DMA((3, 2 * experts)),
-            pltpu.SemaphoreType.DMA((3, 2 * experts)),
-            pltpu.SemaphoreType.DMA((2 * experts,)),
+            pltpu.SemaphoreType.DMA((3, 2 * experts + 1)),
+            pltpu.SemaphoreType.DMA((3, 2 * experts + 1)),
+            pltpu.SemaphoreType.DMA((2 * experts + 1,)),
             pltpu.SemaphoreType.DMA((2,)),
             pltpu.SemaphoreType.DMA((2,)),
         ],

time: 64.6 us -> 64.7 us (level)
  no operation moved by 1% of the time
where the time goes in v5:
time: 64.7 us; the launch traced here: 64.5 us
  Pallas kernels  63 us (97%)
  local copies, waits for them, and re-layouts  0.84 us (1%)
  between operations  0.66 us (1%)
    pallas_call x1, Pallas kernels, fused(): pl.pallas_call(functools.partial(fused_kernel, peers, cap, share), out_sh...  63 us

profile of v5, /device:TPU:0, one launch (start us, length us, event | category | flops | bytes accessed | tf_op | source)
XLA Modules:
  0.0 64.5 jit_solution(16168243062570537215)
XLA Ops:
  0.7 63.0 %fused.1 = bf16[128,2560]{1,0:T(8,128)(2,1)S(1)} custom-call(s32[1]{0:T(128)S(6)} %copy.14.count_ref, s32[1,64]{1,0:T(1,128)} %bitcast.3, s32[1,64]{1,0:T(1,128)} %bitcast.4, s32[1,64]{1,0:T(1,128)} %bitcast.5, s32[64,128]{1,0:T(8,128)} %rows_hbm.1, s32[64,128]{1,0:T(8,128)} %slots_hbm.1, bf16[20,2048,128]{2,1,0:T(8,128)(2,1)} %tables_hbm.1, ...), custom_call_target="tpu_custom_call" | custom-call | tf_op jit(solution)/shard_map/fused/pallas_call | solution.py:788
  63.7 0.8 %copy.15 = bf16[128,2560]{1,0:T(8,128)(2,1)} copy(bf16[128,2560]{1,0:T(8,128)(2,1)S(1)} %fused.1) | data formatting | bytes 1310720
